TPU v7x, 32 devices: a whole 2x2x4 slice. The times are simulated.
32 devices in a mesh: gx: 4 (over z), gy: 4 (over y, x), gz: 2 (over core).
Axes of the slice: x: 2, y: 2, z: 4, core: 2. Of those that a mesh axis runs over, the one named last changes fastest.
Arguments:
- potential: float32 [16, 96, 512], P('gz', 'gx', 'gy'), may hold values from -6 to 6
- tissue_mask: int32 [16, 96, 512], P('gz', 'gx', 'gy'), may hold values from 0 to 2, as said below
- layer_index: int32 [16], P('gz'), may hold values from 0 to 15
- source: float32 [16, 96, 512], P('gz', 'gx', 'gy'), may hold values from -6 to 6
Outputs:
- phi_e: float32 [16, 96, 512], P('gz', 'gx', 'gy')
- residual: float32 [16, 96, 512], P('gz', 'gx', 'gy')
Inputs may be any that keep to these rules, and one draw needn't show every extreme that they name: `tissue_mask`: 0 marks cells outside every medium, 1 bath, 2 tissue.
All inputs are finite; a program needn't handle non-finite values.
Results may differ from a plain program's by a relative error of at most 0.0003.
Values sent between devices are 32-bit elements; how exact they have to be, the bound alone decides.
A program may use at most 128 MiB of HBM per device.

v0:
```python
import functools
import math

import jax
import jax.numpy as jnp
from jax import lax
from jax.experimental import pallas as pl
from jax.experimental.pallas import tpu as pltpu
from jax.sharding import PartitionSpec as P

ITERS = 8
DEPTH = ITERS + 1
LAYERS = 16
AXES = ("gx", "gy", "gz")

OFFSETS = [
    (0, 1, 0),
    (0, 0, 1),
    (1, 0, 0),
    (0, 1, 1),
    (0, 1, -1),
    (1, 1, 0),
    (-1, 1, 0),
    (1, 0, 1),
    (-1, 0, 1),
]
bulk_long = 7.99
bulk_trans = 2.55
intra_long = 1.74
intra_trans = 0.19
bath_sigma = 5.0


def tensor_table(layers, longitudinal, transverse):
    depth = jnp.arange(layers, dtype=jnp.float32) / (layers - 1)
    helix = math.pi / 3.0 * (1.0 - 2.0 * depth)
    tilted = 0.35 * jnp.cos(math.pi * depth)
    fiber_x = jnp.cos(tilted) * jnp.cos(helix)
    fiber_y = jnp.cos(tilted) * jnp.sin(helix)
    fiber_z = jnp.sin(tilted)
    spread = longitudinal - transverse
    s_xx = transverse + spread * fiber_x * fiber_x
    s_yy = transverse + spread * fiber_y * fiber_y
    s_zz = transverse + spread * fiber_z * fiber_z
    s_xy = spread * fiber_x * fiber_y
    s_xz = spread * fiber_x * fiber_z
    s_yz = spread * fiber_y * fiber_z
    columns = [
        s_xx - jnp.abs(s_xy) - jnp.abs(s_xz),
        s_yy - jnp.abs(s_xy) - jnp.abs(s_yz),
        s_zz - jnp.abs(s_xz) - jnp.abs(s_yz),
        jnp.maximum(s_xy, 0.0),
        jnp.maximum(-s_xy, 0.0),
        jnp.maximum(s_xz, 0.0),
        jnp.maximum(-s_xz, 0.0),
        jnp.maximum(s_yz, 0.0),
        jnp.maximum(-s_yz, 0.0),
    ]
    return jnp.stack(columns, axis=1)


def shifted(value, axis, hop):
    count = lax.axis_size(axis)
    pairs = [(i + hop, i) for i in range(count) if 0 <= i + hop < count]
    return lax.ppermute(value, axis, pairs)


def framed(value, axis, dim, multiple):
    count, length = lax.axis_size(axis), value.shape[dim]
    if count == 1:
        return value
    if count == 2 and 2 * length <= length + 2 * DEPTH and multiple == 1:
        other = lax.ppermute(value, axis, [(0, 1), (1, 0)])
        return jnp.concatenate([value, other], axis=dim)
    after, before = [], []
    left, hop = DEPTH, 1
    while left > 0:
        width = min(left, length)
        if hop < count:
            after.append(
                shifted(lax.slice_in_dim(value, 0, width, axis=dim), axis, hop)
            )
            before.insert(
                0, shifted(lax.slice_in_dim(value, length - width, length, axis=dim), axis, -hop)
            )
        else:
            shape = list(value.shape)
            shape[dim] = width
            after.append(jnp.zeros(shape, value.dtype))
            before.insert(0, jnp.zeros(shape, value.dtype))
        left, hop = left - width, hop + 1
    gap = -(length + 2 * DEPTH) % multiple
    shape = list(value.shape)
    shape[dim] = gap
    middle = [jnp.zeros(shape, value.dtype)] if gap else []
    return jnp.concatenate([value] + after + middle + before, axis=dim)


def fields_around(ref, here, above, below, rows, lanes):
    def along_x(value, step):
        return pltpu.roll(value, (-step) % rows, 0)

    def along_y(value, step):
        return pltpu.roll(value, (-step) % lanes, 1)

    for dz, plane in ((0, here), (1, above), (-1, below)):
        value = ref[plane]
        if dz:
            yield (dz, 0, 0), value
        for step in (1, -1):
            yield (dz, step, 0), along_x(value, step)
        for step in (1, -1):
            moved = along_y(value, step)
            yield (dz, 0, step), moved
            if dz == 0:
                for other in (1, -1):
                    yield (0, other, step), along_x(moved, other)


SLOT = {}
for _column, _offset in enumerate(OFFSETS):
    SLOT[_offset] = (_column, 2 * _column)
    SLOT[tuple(-o for o in _offset)] = (_column, 2 * _column + 1)


def grid_kernel(extent, sizes, local, table, mask_in, potential_in, source_in, phi, residual,
                basis, scale, dots, weights, spare, first, second, jac,
                own_row, early, final_row, late, sends, early_recv, late_recv, *extra):
    mask, potential, source = mask_in, potential_in, source_in
    if local:
        fields, pack, from_after, from_before, face_send, face_recv = extra
        mask, potential, source = fields.at[0], fields.at[1], fields.at[2]
    planes, rows, lanes = mask.shape
    nz, nx, ny = extent
    held = jac.shape[1]
    keep = nx + ITERS
    peers = math.prod(sizes)
    me = 0
    for axis, size in zip(AXES, sizes):
        me = me * size + lax.axis_index(axis)

    def device(index):
        return (index // (sizes[1] * sizes[2]), index // sizes[2] % sizes[1], index % sizes[2])

    def peer(k):
        return lax.rem(me + k, peers)

    barrier = pltpu.get_barrier_semaphore()

    def greet(k, carry):
        pl.semaphore_signal(
            barrier, inc=1, device_id=device(peer(k)), device_id_type=pl.DeviceIdType.MESH
        )
        return carry

    lax.fori_loop(1, peers, greet, 0)

    def spread(row, gathered, recv):
        def one(k, carry):
            pltpu.make_async_remote_copy(
                src_ref=row, dst_ref=gathered.at[me], send_sem=sends.at[k],
                recv_sem=recv.at[me], device_id=device(peer(k)),
                device_id_type=pl.DeviceIdType.MESH,
            ).start()
            return carry

        lax.fori_loop(1, peers, one, 0)

    def collect(row, gathered, recv):
        def one(k, carry):
            other = peer(k)
            copy = pltpu.make_async_remote_copy(
                src_ref=row, dst_ref=gathered.at[other], send_sem=sends.at[k],
                recv_sem=recv.at[other], device_id=device(other),
                device_id_type=pl.DeviceIdType.MESH,
            )
            copy.wait_recv()
            copy.wait_send()
            return carry

        lax.fori_loop(1, peers, one, 0)
        gathered[me] = row[...]
        return jnp.sum(gathered[...], axis=0)

    lane = lax.broadcasted_iota(jnp.int32, (1, 128), 1)

    def pick(vector, index):
        return jnp.sum(jnp.where(lane == index, vector, 0.0), axis=1, keepdims=True)

    cells = jnp.zeros((1, ny), jnp.float32)
    injected = jnp.zeros((1, ny), jnp.float32)
    for plane in range(nz):
        own_inside = jnp.where(mask_in[plane, 0:nx, 0:ny] > 0.0, 1.0, 0.0)
        cells = cells + jnp.sum(own_inside, axis=0, keepdims=True)
        injected = injected + jnp.sum(
            own_inside * source_in[plane, 0:nx, 0:ny], axis=0, keepdims=True
        )
    cells = jnp.sum(cells, axis=1, keepdims=True)
    injected = jnp.sum(injected, axis=1, keepdims=True)
    own_row[...] = jnp.where(lane == 0, cells, jnp.where(lane == 1, injected, 0.0))

    def neighbours(plane):
        above = jnp.where(plane + 1 == planes, 0, plane + 1)
        below = jnp.where(plane == 0, planes - 1, plane - 1)
        return above, below

    def store(ref, index, value):
        if held == rows:
            ref[index] = value
        else:
            ref[(*index, slice(0, keep))] = value[:keep]
            ref[(*index, slice(keep, held))] = value[rows - held + keep :]

    def setup(plane, carry):
        above, below = neighbours(plane)
        labels = mask[plane]
        tissue = jnp.where(labels == 2.0, 1.0, 0.0)
        bath = jnp.where(labels == 1.0, 1.0, 0.0)
        inside = tissue + bath
        volts = potential[plane]
        total = jnp.zeros((rows, lanes), jnp.float32)
        image = jnp.zeros((rows, lanes), jnp.float32)
        pairs = zip(
            fields_around(mask, plane, above, below, rows, lanes),
            fields_around(potential, plane, above, below, rows, lanes),
        )
        for (offset, label), (_, volt) in pairs:
            column, slot = SLOT[offset]
            beyond = {0: plane, 1: above, -1: below}[offset[0]]
            link = 0.5
            if offset[0] == 1:
                link = 0.5 * table[plane, 18]
            if offset[0] == -1:
                link = 0.5 * table[below, 18]
            their_tissue = jnp.where(label == 2.0, 1.0, 0.0)
            g_here, g_there = table[plane, column] * link, table[beyond, column] * link
            weight = tissue * g_here
            if column < 3:
                their_bath = jnp.where(label == 1.0, 1.0, 0.0)
                sigma = bath_sigma * link
                weight = inside * (
                    jnp.where(label > 0.0, weight + bath * sigma, 0.0)
                    + (their_tissue * g_there + their_bath * sigma)
                )
            else:
                weight = inside * (jnp.where(label > 0.0, weight, 0.0) + their_tissue * g_there)
            store(weights, (slot, plane), weight)
            total = total + weight
            intra = (table[plane, 9 + column] + table[beyond, 9 + column]) * link
            image = image + (tissue * their_tissue * intra) * (volts - volt)
        bounded = jnp.maximum(total, 1.0)
        jacobi = inside / bounded
        store(jac, (plane,), jacobi + jacobi)
        store(spare, (plane,), inside * (1.0 - jacobi * total))
        store(first, (plane,), jacobi * (inside * source[plane] - image))

        @pl.when(plane < nz)
        def _():
            scale[plane] = (inside * bounded)[:nx, :ny]

        return carry

    def faces(axis, moves):
        size = sizes[AXES.index(axis)]
        place = lax.axis_index(axis)
        copies = []
        for slot, step, src, dst in moves:
            copy = pltpu.make_async_remote_copy(
                src_ref=src, dst_ref=dst, send_sem=face_send.at[slot],
                recv_sem=face_recv.at[slot], device_id={axis: place + step},
                device_id_type=pl.DeviceIdType.MESH,
            )
            copies.append((copy, step))
            pl.when((place + step >= 0) & (place + step < size))(copy.start)
        for copy, step in copies:
            pl.when((place - step >= 0) & (place - step < size))(copy.wait_recv)
            pl.when((place + step >= 0) & (place + step < size))(copy.wait_send)

    if local:
        inputs = (mask_in, potential_in, source_in)
        first_x, last_x = lax.axis_index("gx") == 0, lax.axis_index("gx") == sizes[0] - 1
        first_y, last_y = lax.axis_index("gy") == 0, lax.axis_index("gy") == sizes[1] - 1

        @pl.when(last_x)
        def _():
            fields[:, 0:nz, nx : nx + 16, 0:ny] = jnp.zeros((3, nz, 16, ny), jnp.float32)

        @pl.when(first_x)
        def _():
            fields[:, 0:nz, nx + 16 : nx + 32, 0:ny] = jnp.zeros((3, nz, 16, ny), jnp.float32)

        @pl.when(last_y)
        def _():
            from_after[...] = jnp.zeros(from_after.shape, jnp.float32)

        @pl.when(first_y)
        def _():
            from_before[...] = jnp.zeros(from_before.shape, jnp.float32)

        for index, ref in enumerate(inputs):
            fields[index, 0:nz, 0:nx, 0:ny] = ref[...]
        pl.semaphore_wait(barrier, peers - 1)
        spread(own_row, early, early_recv)
        moves = []
        for index, ref in enumerate(inputs):
            to = fields.at[index, pl.ds(0, nz)]
            moves.append(
                (2 * index, 1, ref.at[:, pl.ds(nx - 16, 16)],
                 to.at[:, pl.ds(nx + 16, 16), pl.ds(0, ny)])
            )
            moves.append(
                (2 * index + 1, -1, ref.at[:, pl.ds(0, 16)],
                 to.at[:, pl.ds(nx, 16), pl.ds(0, ny)])
            )
        faces("gx", moves)
        column = lax.broadcasted_iota(jnp.int32, (rows, ny), 1)

        def packing(plane, carry):
            one = pltpu.roll(fields[1, plane, :, 0:ny], 32, 1)
            two = pltpu.roll(fields[2, plane, :, 0:ny], 64, 1)
            value = fields[0, plane, :, 0:ny]
            value = jnp.where((column >= 23) & (column < 41), one, value)
            pack[plane] = jnp.where((column >= 55) & (column < 73), two, value)
            return carry

        lax.fori_loop(0, nz, packing, 0)
        faces("gy", [(6, 1, pack, from_before), (7, -1, pack, from_after)])

        def unpacking(plane, carry):
            for index in range(3):
                after, before = from_after[plane], from_before[plane]
                if index:
                    after = pltpu.roll(after, ny - 32 * index, 1)
                    before = pltpu.roll(before, ny - 32 * index, 1)
                fields[index, plane, :, ny : 2 * ny] = jnp.where(
                    column < DEPTH, after, jnp.where(column >= ny - DEPTH, before, 0.0)
                )
            return carry

        lax.fori_loop(0, nz, unpacking, 0)
        side = lax.axis_index("gz")
        swap = pltpu.make_async_remote_copy(
            src_ref=fields.at[:, pl.ds(0, nz)], dst_ref=fields.at[:, pl.ds(nz, nz)],
            send_sem=face_send.at[8], recv_sem=face_recv.at[8],
            device_id={"gz": 1 - side}, device_id_type=pl.DeviceIdType.MESH,
        )
        swap.start()
        swap.wait()
        lax.fori_loop(0, planes, setup, 0)
    else:
        lax.fori_loop(0, planes // 2, setup, 0)
        pl.semaphore_wait(barrier, peers - 1)
        spread(own_row, early, early_recv)
        lax.fori_loop(planes // 2, planes, setup, 0)
    totals = collect(own_row, early, early_recv)
    count = pick(totals, 0)
    mean_rhs = pick(totals, 1) / count

    def centre(plane, carry):
        first[plane] = first[plane] - 0.5 * jac[plane] * mean_rhs
        return carry

    lax.fori_loop(0, planes, centre, 0)

    def record(step, now, before):
        rowsum = jnp.zeros((1, ny), jnp.float32)
        square, cross, plain = rowsum, rowsum, rowsum
        for plane in range(nz):
            value = now[plane, 0:nx, 0:ny]
            basis[step, plane] = value
            weighted = value * scale[plane]
            square = square + jnp.sum(weighted * value, axis=0, keepdims=True)
            if step:
                past = basis[step - 1, plane]
                cross = cross + jnp.sum(weighted * past, axis=0, keepdims=True)
            plain = plain + jnp.sum(value, axis=0, keepdims=True)
        if step < ITERS:
            dots[pl.ds(2 * step, 1)] = square
            dots[pl.ds(2 * ITERS + step, 1)] = plain
        if step:
            dots[pl.ds(2 * step - 1, 1)] = cross

    record(0, first, None)

    def apply(now, old, step):
        reach = ITERS - step
        if planes == nz:
            begin, span = 0, nz
        elif planes == sizes[2] * nz:
            begin = planes - lax.axis_index("gz") * reach
            span = min(planes, nz + reach)
        else:
            begin, span = planes - reach, nz + 2 * reach

        def one(index, carry):
            plane = lax.rem(begin + index, planes)
            above, below = neighbours(plane)
            total = jnp.zeros((held, lanes), jnp.float32)
            for offset, value in fields_around(now, plane, above, below, held, lanes):
                total = total + weights[SLOT[offset][1], plane] * value
            if step == 1:
                old[plane] = 0.5 * jac[plane] * total + spare[plane] * now[plane]
            else:
                old[plane] = (
                    jac[plane] * total + 2.0 * spare[plane] * now[plane] - old[plane]
                )
            return carry

        lax.fori_loop(0, span, one, 0)

    now, old = first, second
    for step in range(1, ITERS + 1):
        apply(now, old, step)
        now, old = old, now
        record(step, now, old)

    partial = jnp.sum(dots[...], axis=1, keepdims=True)
    diagonal = lax.broadcasted_iota(jnp.int32, (3 * ITERS, 128), 0) == lax.broadcasted_iota(
        jnp.int32, (3 * ITERS, 128), 1
    )
    final_row[...] = jnp.sum(jnp.where(diagonal, partial, 0.0), axis=0, keepdims=True)
    spread(final_row, late, late_recv)
    sums = collect(final_row, late, late_recv)

    def left(vector):
        return pltpu.roll(vector, 127, 1)

    def right(vector):
        return pltpu.roll(vector, 1, 1)

    mu0, mu1 = pick(sums, 0), pick(sums, 1)
    mu = jnp.where(lane < 2, sums, 2.0 * sums - jnp.where(lane % 2 == 0, mu0, mu1))
    mu = jnp.where(lane < 2 * ITERS, mu, 0.0)
    ones = pltpu.roll(sums, 128 - 2 * ITERS, 1)
    y = jnp.where(lane == 0, 1.0, 0.0)
    p = y
    m_y, m_p = mu, mu
    x = jnp.zeros((1, 128), jnp.float32)
    rz = mu0
    for step in range(ITERS):
        h_p = p - 0.5 * (left(p) + jnp.where(lane == 1, 2.0, 1.0) * right(p))
        h_p = jnp.where(lane <= ITERS, h_p, 0.0)
        before = jnp.where(lane == 0, left(m_p), right(m_p))
        m_h = m_p - 0.5 * (left(m_p) + before)
        alpha = rz / jnp.sum(jnp.where(lane < ITERS, p * m_h, 0.0), axis=1, keepdims=True)
        x = x + alpha * p
        y = y - alpha * h_p
        m_y = m_y - alpha * m_h
        if step + 1 < ITERS:
            rz_next = jnp.sum(jnp.where(lane < ITERS, y * m_y, 0.0), axis=1, keepdims=True)
            beta = rz_next / rz
            p = y + beta * p
            m_p = m_y + beta * m_p
            rz = rz_next
    mean = jnp.sum(jnp.where(lane < ITERS, x * ones, 0.0), axis=1, keepdims=True) / count
    xs = [pick(x, j) for j in range(ITERS)]
    ys = [pick(y, j) for j in range(ITERS + 1)]

    def one(plane, carry):
        weight = scale[plane]
        total = jnp.where(weight > 0.0, -mean, 0.0)
        rest = ys[ITERS] * basis[ITERS, plane]
        for j in range(ITERS):
            value = basis[j, plane]
            total = total + xs[j] * value
            rest = rest + ys[j] * value
        phi[plane] = total
        residual[plane] = weight * rest
        return carry

    lax.fori_loop(0, nz, one, 0)


def body(potential, tissue_mask, layer_index, source):
    extent = tissue_mask.shape
    nz = extent[0]
    labels = tissue_mask.astype(jnp.float32)
    sizes = tuple(lax.axis_size(axis) for axis in AXES)
    local = (
        sizes[2] == 2 and nz <= DEPTH and extent[1] % 8 == 0 and extent[1] >= 16
        and extent[2] == 128
    )
    if local:
        operands = (labels, potential, source)
        frame = (2 * nz, extent[1] + 32, 2 * extent[2])
    else:
        packed = jnp.stack([labels, potential, source], axis=1)
        packed = framed(packed, "gz", 0, 1)
        packed = framed(packed, "gx", 2, 8)
        packed = framed(packed, "gy", 3, 128)
        operands = (packed[:, 0], packed[:, 1], packed[:, 2])
        frame = operands[0].shape
    layers = framed(layer_index, "gz", 0, 1)
    planes = layers.shape[0]
    selector = (layers[:, None] == jnp.arange(LAYERS, dtype=jnp.int32)[None, :]).astype(
        jnp.float32
    )
    tables = jnp.concatenate(
        [
            tensor_table(LAYERS, bulk_long, bulk_trans),
            tensor_table(LAYERS, intra_long, intra_trans),
        ],
        axis=1,
    )
    table = jnp.dot(selector, tables, precision=lax.Precision.HIGHEST)
    size = lax.axis_size("gz")
    link = jnp.ones((planes, 1), jnp.float32)
    if planes == size * nz:
        place = (lax.axis_index("gz") * nz + jnp.arange(planes)) % planes
        link = (place + 1 < planes).astype(jnp.float32)[:, None]
    table = jnp.concatenate([table, link], axis=1)
    smem = pl.BlockSpec(memory_space=pltpu.SMEM)
    vmem = pl.BlockSpec(memory_space=pltpu.VMEM)
    compact = frame
    if extent[1] % 8 == 0 and ITERS % 8 == 0 and frame[1] > extent[1] + 2 * ITERS:
        compact = (planes, extent[1] + 2 * ITERS, frame[2])
    strip = pltpu.VMEM((nz,) + (frame[1], extent[2]), jnp.float32)
    extra = []
    if local:
        extra = [pltpu.VMEM((3,) + frame, jnp.float32), strip, strip, strip]
        extra += [pltpu.SemaphoreType.DMA((9,))] * 2
    peers = math.prod(sizes)
    row = pltpu.VMEM((1, 128), jnp.float32)
    gathered = pltpu.VMEM((peers, 1, 128), jnp.float32)
    return tuple(
        pl.pallas_call(
            functools.partial(grid_kernel, extent, sizes, local),
            out_shape=(jax.ShapeDtypeStruct(extent, jnp.float32),) * 2,
            in_specs=[smem, vmem, vmem, vmem],
            out_specs=(vmem, vmem),
            scratch_shapes=[
                pltpu.VMEM((ITERS + 1,) + extent, jnp.float32),
                pltpu.VMEM(extent, jnp.float32),
                pltpu.VMEM((3 * ITERS, extent[2]), jnp.float32),
                pltpu.VMEM((18,) + compact, jnp.float32),
            ]
            + [pltpu.VMEM(compact, jnp.float32)] * 4
            + [row, gathered, row, gathered]
            + [pltpu.SemaphoreType.DMA((peers,))] * 3
            + extra,
            compiler_params=pltpu.CompilerParams(
                vmem_limit_bytes=60 * 1024 * 1024, collective_id=0, has_side_effects=True
            ),
        )(table, *operands)
    )


def solution(mesh):
    placed = (P("gz", "gx", "gy"), P("gz", "gx", "gy"), P("gz"), P("gz", "gx", "gy"))
    return jax.shard_map(
        body,
        mesh=mesh,
        in_specs=placed,
        out_specs=(P("gz", "gx", "gy"), P("gz", "gx", "gy")),
        check_vma=False,
    )
```

profile of v0, /device:TPU:0, one launch (start us, length us, event | category | flops | bytes accessed | tf_op | source)
XLA Modules:
  0.0 68.1 jit_solution(7517303125009621998)
XLA Ops:
  0.6 0.6 collective-permute-start
  1.2 0.1 broadcast_maximum_fusion.4
  1.3 0.1 broadcast_maximum_fusion.2
  1.4 0.1 broadcast_maximum_fusion
  1.5 0.1 negate_maximum_fusion.5
  1.6 0.1 negate_maximum_fusion.3
  1.7 0.1 negate_maximum_fusion.2
  1.8 0.1 negate_maximum_fusion
  1.9 0.1 fusion.21
  2.0 0.1 fusion.11
  2.1 1.5 %convert_element_type.15.mask_in = f32[8,24,128]{2,1,0:T(8,128)} convert(s32[8,24,128]{2,1,0:T(8,128)} %param.5) | non-fusion elementwise | flops 24576 | bytes 196608 | tf_op jit(solution)/shard_map/convert_element_type | solution.py:477
  3.7 0.0 copy-start.1
  3.7 0.1 concatenate.10
  3.7 0.0 collective-permute-done
  3.7 0.6 copy-done.1
  4.3 0.1 pad_add_fusion
  4.4 0.2 fusion.7
  4.6 0.7 %pad_maximum_fusion.table = f32[16,19]{1,0:T(8,128)} fusion(f32[16,1]{1,0:T(8,128)S(1)} %fusion.5, f32[16,18]{1,0:T(8,128)S(1)} %fusion.7), kind=kLoop, calls=%fused_computation.6 | loop fusion | flops 304 | bytes 2432 | tf_op jit(solution)/shard_map/concatenate | solution.py:511
  5.3 60.6 %shard_map.59 = (f32[8,24,128]{2,1,0:T(8,128)}, f32[8,24,128]{2,1,0:T(8,128)}) custom-call(f32[16,19]{1,0:T(8,128)} %pad_maximum_fusion.table, f32[8,24,128]{2,1,0:T(8,128)} %convert_element_type.15.mask_in, f32[8,24,128]{2,1,0:T(8,128)} %potential_in.1, f32[8,24,128]{2,1,0:T(8,128)} %source_in.1), custom_call_target="tpu_custom_call" | custom-call | tf_op jit(solution)/shard_map/pallas_call | solution.py:526
  65.9 0.0 copy-start
  65.9 1.6 %copy.8 = f32[8,24,128]{2,1,0:T(8,128)} copy(f32[8,24,128]{2,1,0:T(8,128)} %get-tuple-element.22) | data formatting | bytes 196608
  67.5 0.0 copy-done
  67.5 0.6 copy.9
  (1 shorter events, 0.0 us)
Async XLA Ops:
  0.6 3.1 %collective-permute-start = (s32[8]{0:T(128)}, s32[8]{0:T(128)S(1)}, u32[]{:S(2)}, u32[]{:S(2)}) collective-permute-start(s32[8]{0:T(128)} %param.6), channel_id=1, source_target_pairs={{0,1},{1,0},{2,3},{3,2},{4,5},{5,4},{6,7},{7,6},{8,9},{9,8},{10,11... | collective-permute-start | bytes 104 | tf_op jit(solution)/shard_map/ppermute | solution.py:73
  3.7 0.7 copy-start.1
  65.9 1.6 %copy-start = (f32[8,24,128]{2,1,0:T(8,128)S(1)}, f32[8,24,128]{2,1,0:T(8,128)}, u32[]{:S(2)}) copy-start(f32[8,24,128]{2,1,0:T(8,128)} %get-tuple-element.23) | copy-start | bytes 294916
where the time goes:
time: 68.4 us; the launch traced here: 68.1 us
  Pallas kernels  60.6 us (89%)
  other arithmetic  3.19 us (5%)
  local copies, waits for them, and re-layouts  2.87 us (4%)
  between operations  0.7 us (1%)
    pallas_call x1, Pallas kernels, body(): pl.pallas_call(functools.partial(grid_kernel, extent, sizes, local), out_...  60.6 us
    unnamed x6, local copies, waits for them, and re-layouts  2.8 us
    convert_element_type x1, other arithmetic, body(): labels = tissue_mask.astype(jnp.float32)  1.54 us
  transfers between devices with their start and end apart: 1, of which 0 were waited for; matrix products, arithmetic and copies ran while one was open for 4% of the time, Pallas kernels for 0%

commit v1 on v0

--- a/solution.py
+++ b/solution.py
@@ -7,6 +7,7 @@
 from jax.experimental import pallas as pl
 from jax.experimental.pallas import tpu as pltpu
 from jax.sharding import PartitionSpec as P
+import numpy as np
 
 ITERS = 8
 DEPTH = ITERS + 1
@@ -123,13 +124,10 @@
     SLOT[tuple(-o for o in _offset)] = (_column, 2 * _column + 1)
 
 
-def grid_kernel(extent, sizes, local, table, mask_in, potential_in, source_in, phi, residual,
+def grid_kernel(extent, sizes, table, mask_in, potential_in, source_in, phi, residual,
                 basis, scale, dots, weights, spare, first, second, jac,
-                own_row, early, final_row, late, sends, early_recv, late_recv, *extra):
+                own_row, early, final_row, late, sends, early_recv, late_recv):
     mask, potential, source = mask_in, potential_in, source_in
-    if local:
-        fields, pack, from_after, from_before, face_send, face_recv = extra
-        mask, potential, source = fields.at[0], fields.at[1], fields.at[2]
     planes, rows, lanes = mask.shape
     nz, nx, ny = extent
     held = jac.shape[1]
@@ -260,98 +258,10 @@
 
         return carry
 
-    def faces(axis, moves):
-        size = sizes[AXES.index(axis)]
-        place = lax.axis_index(axis)
-        copies = []
-        for slot, step, src, dst in moves:
-            copy = pltpu.make_async_remote_copy(
-                src_ref=src, dst_ref=dst, send_sem=face_send.at[slot],
-                recv_sem=face_recv.at[slot], device_id={axis: place + step},
-                device_id_type=pl.DeviceIdType.MESH,
-            )
-            copies.append((copy, step))
-            pl.when((place + step >= 0) & (place + step < size))(copy.start)
-        for copy, step in copies:
-            pl.when((place - step >= 0) & (place - step < size))(copy.wait_recv)
-            pl.when((place + step >= 0) & (place + step < size))(copy.wait_send)
-
-    if local:
-        inputs = (mask_in, potential_in, source_in)
-        first_x, last_x = lax.axis_index("gx") == 0, lax.axis_index("gx") == sizes[0] - 1
-        first_y, last_y = lax.axis_index("gy") == 0, lax.axis_index("gy") == sizes[1] - 1
-
-        @pl.when(last_x)
-        def _():
-            fields[:, 0:nz, nx : nx + 16, 0:ny] = jnp.zeros((3, nz, 16, ny), jnp.float32)
-
-        @pl.when(first_x)
-        def _():
-            fields[:, 0:nz, nx + 16 : nx + 32, 0:ny] = jnp.zeros((3, nz, 16, ny), jnp.float32)
-
-        @pl.when(last_y)
-        def _():
-            from_after[...] = jnp.zeros(from_after.shape, jnp.float32)
-
-        @pl.when(first_y)
-        def _():
-            from_before[...] = jnp.zeros(from_before.shape, jnp.float32)
-
-        for index, ref in enumerate(inputs):
-            fields[index, 0:nz, 0:nx, 0:ny] = ref[...]
-        pl.semaphore_wait(barrier, peers - 1)
-        spread(own_row, early, early_recv)
-        moves = []
-        for index, ref in enumerate(inputs):
-            to = fields.at[index, pl.ds(0, nz)]
-            moves.append(
-                (2 * index, 1, ref.at[:, pl.ds(nx - 16, 16)],
-                 to.at[:, pl.ds(nx + 16, 16), pl.ds(0, ny)])
-            )
-            moves.append(
-                (2 * index + 1, -1, ref.at[:, pl.ds(0, 16)],
-                 to.at[:, pl.ds(nx, 16), pl.ds(0, ny)])
-            )
-        faces("gx", moves)
-        column = lax.broadcasted_iota(jnp.int32, (rows, ny), 1)
-
-        def packing(plane, carry):
-            one = pltpu.roll(fields[1, plane, :, 0:ny], 32, 1)
-            two = pltpu.roll(fields[2, plane, :, 0:ny], 64, 1)
-            value = fields[0, plane, :, 0:ny]
-            value = jnp.where((column >= 23) & (column < 41), one, value)
-            pack[plane] = jnp.where((column >= 55) & (column < 73), two, value)
-            return carry
-
-        lax.fori_loop(0, nz, packing, 0)
-        faces("gy", [(6, 1, pack, from_before), (7, -1, pack, from_after)])
-
-        def unpacking(plane, carry):
-            for index in range(3):
-                after, before = from_after[plane], from_before[plane]
-                if index:
-                    after = pltpu.roll(after, ny - 32 * index, 1)
-                    before = pltpu.roll(before, ny - 32 * index, 1)
-                fields[index, plane, :, ny : 2 * ny] = jnp.where(
-                    column < DEPTH, after, jnp.where(column >= ny - DEPTH, before, 0.0)
-                )
-            return carry
-
-        lax.fori_loop(0, nz, unpacking, 0)
-        side = lax.axis_index("gz")
-        swap = pltpu.make_async_remote_copy(
-            src_ref=fields.at[:, pl.ds(0, nz)], dst_ref=fields.at[:, pl.ds(nz, nz)],
-            send_sem=face_send.at[8], recv_sem=face_recv.at[8],
-            device_id={"gz": 1 - side}, device_id_type=pl.DeviceIdType.MESH,
-        )
-        swap.start()
-        swap.wait()
-        lax.fori_loop(0, planes, setup, 0)
-    else:
-        lax.fori_loop(0, planes // 2, setup, 0)
-        pl.semaphore_wait(barrier, peers - 1)
-        spread(own_row, early, early_recv)
-        lax.fori_loop(planes // 2, planes, setup, 0)
+    lax.fori_loop(0, planes // 2, setup, 0)
+    pl.semaphore_wait(barrier, peers - 1)
+    spread(own_row, early, early_recv)
+    lax.fori_loop(planes // 2, planes, setup, 0)
     totals = collect(own_row, early, early_recv)
     count = pick(totals, 0)
     mean_rhs = pick(totals, 1) / count
@@ -471,25 +381,17 @@
     lax.fori_loop(0, nz, one, 0)
 
 
-def body(potential, tissue_mask, layer_index, source):
+def general_body(potential, tissue_mask, layer_index, source):
     extent = tissue_mask.shape
     nz = extent[0]
     labels = tissue_mask.astype(jnp.float32)
     sizes = tuple(lax.axis_size(axis) for axis in AXES)
-    local = (
-        sizes[2] == 2 and nz <= DEPTH and extent[1] % 8 == 0 and extent[1] >= 16
-        and extent[2] == 128
-    )
-    if local:
-        operands = (labels, potential, source)
-        frame = (2 * nz, extent[1] + 32, 2 * extent[2])
-    else:
-        packed = jnp.stack([labels, potential, source], axis=1)
-        packed = framed(packed, "gz", 0, 1)
-        packed = framed(packed, "gx", 2, 8)
-        packed = framed(packed, "gy", 3, 128)
-        operands = (packed[:, 0], packed[:, 1], packed[:, 2])
-        frame = operands[0].shape
+    packed = jnp.stack([labels, potential, source], axis=1)
+    packed = framed(packed, "gz", 0, 1)
+    packed = framed(packed, "gx", 2, 8)
+    packed = framed(packed, "gy", 3, 128)
+    operands = (packed[:, 0], packed[:, 1], packed[:, 2])
+    frame = operands[0].shape
     layers = framed(layer_index, "gz", 0, 1)
     planes = layers.shape[0]
     selector = (layers[:, None] == jnp.arange(LAYERS, dtype=jnp.int32)[None, :]).astype(
@@ -514,17 +416,12 @@
     compact = frame
     if extent[1] % 8 == 0 and ITERS % 8 == 0 and frame[1] > extent[1] + 2 * ITERS:
         compact = (planes, extent[1] + 2 * ITERS, frame[2])
-    strip = pltpu.VMEM((nz,) + (frame[1], extent[2]), jnp.float32)
-    extra = []
-    if local:
-        extra = [pltpu.VMEM((3,) + frame, jnp.float32), strip, strip, strip]
-        extra += [pltpu.SemaphoreType.DMA((9,))] * 2
     peers = math.prod(sizes)
     row = pltpu.VMEM((1, 128), jnp.float32)
     gathered = pltpu.VMEM((peers, 1, 128), jnp.float32)
     return tuple(
         pl.pallas_call(
-            functools.partial(grid_kernel, extent, sizes, local),
+            functools.partial(grid_kernel, extent, sizes),
             out_shape=(jax.ShapeDtypeStruct(extent, jnp.float32),) * 2,
             in_specs=[smem, vmem, vmem, vmem],
             out_specs=(vmem, vmem),
@@ -536,13 +433,695 @@
             ]
             + [pltpu.VMEM(compact, jnp.float32)] * 4
             + [row, gathered, row, gathered]
-            + [pltpu.SemaphoreType.DMA((peers,))] * 3
-            + extra,
+            + [pltpu.SemaphoreType.DMA((peers,))] * 3,
             compiler_params=pltpu.CompilerParams(
                 vmem_limit_bytes=60 * 1024 * 1024, collective_id=0, has_side_effects=True
             ),
         )(table, *operands)
     )
+
+
+GROUP = 16
+TERMS_SAME = [(0, 1), (0, -1), (1, 0), (-1, 0), (1, 1), (1, -1), (-1, 1), (-1, -1)]
+TERMS_SIDE = [(0, 0), (0, 1), (0, -1), (1, 0), (-1, 0)]
+LEVEL = [0, 1, 3, 4]
+STEEP = [(0, 0), (1, 0), (-1, 0), (0, 1), (0, -1)]
+COEFS = 2 * len(LEVEL) + 2 * (1 + 3 * len(STEEP))
+
+
+def numpy_table(longitudinal, transverse):
+    depth = np.arange(LAYERS, dtype=np.float64) / (LAYERS - 1)
+    helix = math.pi / 3.0 * (1.0 - 2.0 * depth)
+    tilted = 0.35 * np.cos(math.pi * depth)
+    fiber = (np.cos(tilted) * np.cos(helix), np.cos(tilted) * np.sin(helix), np.sin(tilted))
+    spread = longitudinal - transverse
+    s_xx, s_yy, s_zz = (transverse + spread * f * f for f in fiber)
+    s_xy = spread * fiber[0] * fiber[1]
+    s_xz = spread * fiber[0] * fiber[2]
+    s_yz = spread * fiber[1] * fiber[2]
+    columns = [s_xx - abs(s_xy) - abs(s_xz), s_yy - abs(s_xy) - abs(s_yz), s_zz - abs(s_xz) - abs(s_yz)]
+    for value in (s_xy, s_xz, s_yz):
+        columns += [np.maximum(value, 0.0), np.maximum(-value, 0.0)]
+    return np.stack(columns, axis=1)
+
+
+HALF_TABLE = 0.5 * np.concatenate(
+    [numpy_table(bulk_long, bulk_trans), numpy_table(intra_long, intra_trans)], axis=1
+)
+
+
+def lane_roll(value, step):
+    return pltpu.roll(value, step % value.shape[1], 1)
+
+
+def row_roll(value, step):
+    return pltpu.roll(value, step % value.shape[0], 0)
+
+
+def tiled(value, rows):
+    return jnp.concatenate([value] * (rows // value.shape[0]), axis=0)
+
+
+def column_of(dz, dx, dy, side):
+    same, flipped = SLOT[(dz, dx, dy)][0], SLOT[(-dz, dx, dy)][0]
+    return same if same == flipped else same + side * (flipped - same)
+
+
+def fast_kernel(extent, sizes, potential_in, mask_in, layers_in, source_in, phi, residual,
+                fields, labels, packs, edge_send, edge_recv, from_after, from_before, strips,
+                derived, weights, basis, moved, beside, jac, spare, scale, coef_lanes, dots,
+                early_row, early_all, line_row, line_all, final_row, final_all,
+                table, coefs, layers_own, layers_far, layers,
+                loads, halo_send, halo_recv, sum_send, sum_recv):
+    nz, nx, ny = extent
+    planes, held, deep = 2 * nz, nx + 16, nx + 32
+    own = slice(8, 8 + nx)
+    place = tuple(lax.axis_index(axis) for axis in AXES)
+    gx, gy, side = place
+    first_x, last_x = gx == 0, gx == sizes[0] - 1
+    first_y, last_y = gy == 0, gy == sizes[1] - 1
+
+    def exists(dx, dy):
+        return (gx + dx >= 0) & (gx + dx < sizes[0]) & (gy + dy >= 0) & (gy + dy < sizes[1])
+
+    def around(a, b, c):
+        return tuple(
+            lax.rem(here + step, size) if step else here
+            for here, step, size in zip(place, (a, b, c), sizes)
+        )
+
+    slab = [(0, b, c) for b in range(sizes[1]) for c in range(sizes[2])]
+    line = [(a, 0, 0) for a in range(sizes[0])]
+    everyone = [(a, b, c) for a, _, _ in line for _, b, c in slab]
+    corners = [(dx, dy) for dx in (1, -1) for dy in (1, -1)]
+
+    def flip(slot, turned):
+        return slot + turned * (nz - 1 - 2 * slot)
+
+    barrier = pltpu.get_barrier_semaphore()
+
+    def greet(target):
+        pl.semaphore_signal(
+            barrier, inc=1, device_id=target, device_id_type=pl.DeviceIdType.MESH
+        )
+
+    expected = len(slab) + len(line) - 2
+    for step in slab[1:] + line[1:]:
+        greet(around(*step))
+    for dx, dy in corners:
+        pl.when(exists(dx, dy))(lambda: greet((gx + dx, gy + dy, side)))
+        expected = expected + jnp.where(exists(dx, dy), 1, 0)
+
+    get_layers = pltpu.make_async_copy(layers_in, layers_own, loads.at[0])
+    get_mask = pltpu.make_async_copy(mask_in, labels, loads.at[1])
+    get_layers.start()
+    get_mask.start()
+    whole = []
+    for index, ref in ((1, potential_in), (2, source_in)):
+        for plane in range(nz):
+            pltpu.make_async_copy(
+                ref.at[plane], fields.at[index, flip(plane, side), own], loads.at[1 + index]
+            ).start()
+        whole.append(pltpu.make_async_copy(ref, fields.at[index, 0:nz, own], loads.at[1 + index]))
+
+    def clear(when, ref, index):
+        @pl.when(when)
+        def _():
+            ref[index] = jnp.zeros(ref.at[index].shape, jnp.float32)
+
+    every = slice(None)
+    clear(first_x, fields, (every, slice(0, nz), slice(0, 8)))
+    clear(last_x, fields, (every, slice(0, nz), slice(8 + nx, held)))
+    clear(first_x, edge_recv, (0, 0))
+    clear(last_x, edge_recv, (0, 1))
+    for ref, edge in ((from_after, last_y), (from_before, first_y)):
+        clear(edge, ref, (every,))
+        clear(first_x, ref, (every, slice(0, 16)))
+        clear(last_x, ref, (every, slice(16 + nx, deep)))
+    for layer in range(LAYERS):
+        for column in range(18):
+            table[layer, column] = jnp.float32(HALF_TABLE[layer, column])
+
+    def lanes_of(rows):
+        lane = lax.broadcasted_iota(jnp.int32, (rows, ny), 1)
+        return lane, lane // GROUP, lane % GROUP
+
+    get_layers.wait()
+    get_mask.wait()
+    for plane in range(nz):
+        fields[0, flip(plane, side), own] = labels[plane].astype(jnp.float32)
+    for copy in whole:
+        copy.wait()
+
+    _, group, inner = lanes_of(nx)
+
+    def packed(values, shift):
+        total = values[0]
+        total = lane_roll(total, shift)
+        for g in range(1, nz):
+            total = jnp.where(group == g, lane_roll(values[g], GROUP * g + shift), total)
+        return total
+
+    for index in range(3):
+        values = [fields[index, slot, own] for slot in range(nz)]
+        packs[index] = packed(values, 8)
+        if index < 2:
+            packs[3 + index] = jnp.where(inner == 15, packed(values, 7), packed(values, 9))
+            for slot in range(nz):
+                edge_send[0, index, slot : slot + 1] = values[slot][8:9]
+                edge_send[1, index, slot : slot + 1] = values[slot][nx - 9 : nx - 8]
+
+    pl.semaphore_wait(barrier, expected)
+
+    def link(number, src, dst, target):
+        return pltpu.make_async_remote_copy(
+            src_ref=src, dst_ref=dst, send_sem=halo_send.at[number],
+            recv_sem=halo_recv.at[number], device_id=target,
+            device_id_type=pl.DeviceIdType.MESH,
+        )
+
+    moves = []
+
+    def move(dx, dy, src, dst):
+        copy = link(len(moves), src, dst, (gx + dx, gy + dy, side))
+        pl.when(exists(dx, dy))(copy.start)
+        moves.append((exists(-dx, -dy), exists(dx, dy), copy))
+
+    for dx, dy in corners:
+        into = from_before if dy == 1 else from_after
+        if dx == 1:
+            move(dx, dy, packs.at[:, nx - 16 : nx], into.at[:, 0:16])
+        else:
+            move(dx, dy, packs.at[:, 0:16], into.at[:, 16 + nx : deep])
+    move(0, 1, packs, from_before.at[:, 16 : 16 + nx])
+    move(0, -1, packs, from_after.at[:, 16 : 16 + nx])
+    move(1, 0, edge_send.at[1], edge_recv.at[0, 0])
+    move(-1, 0, edge_send.at[0], edge_recv.at[0, 1])
+    move(1, 0, fields.at[:, 0:nz, nx : nx + 8], fields.at[:, 0:nz, 0:8])
+    move(-1, 0, fields.at[:, 0:nz, 8:16], fields.at[:, 0:nz, 8 + nx : held])
+    other = (gx, gy, 1 - side)
+    base = len(moves)
+    swaps = [
+        link(base, layers_own, layers_far, other),
+        link(base + 1, fields.at[:, 0:nz, own], fields.at[:, nz:planes, own], other),
+    ]
+    for copy in swaps:
+        copy.start()
+
+    def spread(number, row, gathered, targets):
+        for index, step in enumerate(targets):
+            if index:
+                pltpu.make_async_remote_copy(
+                    src_ref=row, dst_ref=gathered.at[index], send_sem=sum_send.at[number],
+                    recv_sem=sum_recv.at[number], device_id=around(*step),
+                    device_id_type=pl.DeviceIdType.MESH,
+                ).start()
+
+    def collect(number, row, gathered, targets):
+        arrived = gathered.at[pl.ds(1, len(targets) - 1)]
+        pltpu.make_async_copy(arrived, arrived, sum_recv.at[number]).wait()
+        pltpu.make_async_copy(arrived, arrived, sum_send.at[number]).wait()
+        gathered[0] = row[...]
+        return jnp.sum(gathered[...], axis=0)
+
+    lane = lax.broadcasted_iota(jnp.int32, (1, ny), 1)
+
+    def pick(vector, index):
+        return jnp.sum(jnp.where(lane == index, vector, 0.0), axis=1, keepdims=True)
+
+    cells = jnp.zeros((8, ny), jnp.float32)
+    injected = cells
+    for slot in range(nz):
+        for row in range(8, 8 + nx, 8):
+            inside = jnp.where(fields[0, slot, row : row + 8] > 0.0, 1.0, 0.0)
+            cells = cells + inside
+            injected = injected + inside * fields[2, slot, row : row + 8]
+    cells = jnp.sum(jnp.sum(cells, axis=0, keepdims=True), axis=1, keepdims=True)
+    injected = jnp.sum(jnp.sum(injected, axis=0, keepdims=True), axis=1, keepdims=True)
+    early_row[...] = jnp.where(lane == 0, cells, jnp.where(lane == 1, injected, 0.0))
+    spread(0, early_row, early_all, slab)
+
+    swaps[0].wait()
+    for slot in range(nz):
+        layers[slot] = layers_own[flip(slot, side)]
+        layers[nz + slot] = layers_far[flip(slot, 1 - side)]
+
+    def slot_of(j):
+        return jnp.where(j < nz, j, 3 * nz - 1 - j)
+
+    def coefficients(slot, carry):
+        j = slot_of(slot)
+        layer = layers[slot]
+        for n, k in enumerate(LEVEL):
+            coefs[slot, 2 * n] = table[layer, k]
+            coefs[slot, 2 * n + 1] = 2.0 * table[layer, 9 + k]
+        for half, dz in enumerate((1, -1)):
+            near = (j + dz >= 0) & (j + dz < planes)
+            there = layers[slot_of(jnp.where(near, j + dz, j))]
+            open_ = jnp.where(near, 1.0, 0.0).astype(jnp.float32)
+            start = 2 * len(LEVEL) + half * (1 + 3 * len(STEEP))
+            coefs[slot, start] = 0.5 * bath_sigma * open_
+            for n, (dx, dy) in enumerate(STEEP):
+                k = column_of(dz, dx, dy, side)
+                coefs[slot, start + 1 + 3 * n] = table[layer, k] * open_
+                coefs[slot, start + 2 + 3 * n] = table[there, k] * open_
+                coefs[slot, start + 3 + 3 * n] = (table[layer, 9 + k] + table[there, 9 + k]) * open_
+        return carry
+
+    lax.fori_loop(0, planes, coefficients, 0)
+    _, group8, _ = lanes_of(8)
+
+    def widen(n, carry):
+        for q in range(2):
+            value = jnp.full((8, ny), coefs[q * nz, n], jnp.float32)
+            for g in range(1, nz):
+                value = jnp.where(group8 == g, coefs[q * nz + g, n], value)
+            coef_lanes[q, n] = value
+        return carry
+
+    lax.fori_loop(0, COEFS, widen, 0)
+
+    line_row[...] = collect(0, early_row, early_all, slab)
+    spread(1, line_row, line_all, line)
+
+    for receives, _, copy in moves:
+        pl.when(receives)(copy.wait_recv)
+    _, _, inner_deep = lanes_of(deep)
+    for index in range(5):
+        strips[index, 0] = jnp.where(inner_deep < 8, from_before[index], from_after[index])
+    late = [
+        (strips.at[:, 0], strips.at[:, 1]),
+        (edge_recv.at[0], edge_recv.at[1]),
+        (fields.at[:, 0:nz, 0:8], fields.at[:, nz:planes, 0:8]),
+        (fields.at[:, 0:nz, 8 + nx : held], fields.at[:, nz:planes, 8 + nx : held]),
+    ]
+    for number, (src, dst) in enumerate(late):
+        swaps.append(link(base + 2 + number, src, dst, other))
+        swaps[-1].start()
+
+    lane_deep, group_deep, inner_deep = lanes_of(deep)
+
+    def sides(value, strip, g):
+        ring = lane_roll(strip, -(GROUP * g + 8))
+        after = lane_roll(jnp.where(lane_of == 0, ring, value), -1)
+        before = lane_roll(jnp.where(lane_of == ny - 1, ring, value), 1)
+        return after, before
+
+    def inserted(values):
+        total = lane_roll(values[0], 8)
+        for g in range(1, len(values)):
+            total = jnp.where(group_of == g, lane_roll(values[g], GROUP * g + 8), total)
+        return total
+
+    def stored(number, slot, label, volts):
+        derived[3 * number, slot] = jnp.where(label == 2.0, 1.0, 0.0)
+        derived[3 * number + 1, slot] = jnp.where(label > 0.0, 1.0, 0.0)
+        derived[3 * number + 2, slot] = volts
+
+    lane_of, group_of = lane_deep, group_deep
+
+    def framed_plane(index, q, g):
+        before = jnp.broadcast_to(edge_recv[q, 0, index, g : g + 1], (8, ny))
+        after = jnp.broadcast_to(edge_recv[q, 1, index, g : g + 1], (8, ny))
+        return jnp.concatenate([before, fields[index, q * nz + g], after], axis=0)
+
+    for q in range(2):
+        if q:
+            for copy in swaps[1:]:
+                copy.wait_recv()
+        found = [[], []]
+        for g in range(nz):
+            parts = []
+            for index in range(2):
+                value = framed_plane(index, q, g)
+                found[index].append(value)
+                parts.append((value,) + sides(value, strips[index, q], g))
+            for number in range(3):
+                stored(number, q * nz + g, parts[0][number], parts[1][number])
+        parts = []
+        for index in range(2):
+            value, edge = strips[index, q], strips[3 + index, q]
+            mixed = inserted(found[index])
+            after = lane_roll(jnp.where(inner_deep == 8, mixed, value), -1)
+            before = lane_roll(jnp.where(inner_deep == 7, mixed, value), 1)
+            after = jnp.where(inner_deep == 15, edge, after)
+            before = jnp.where(inner_deep == 0, edge, before)
+            parts.append((value, after, before))
+        for number in range(3):
+            stored(number, planes + q, parts[0][number], parts[1][number])
+
+    def across(lower, upper):
+        up0 = jnp.where(group_of == nz - 1, upper, lane_roll(lower, -GROUP))
+        up1 = lane_roll(upper, GROUP)
+        down0 = lane_roll(lower, GROUP)
+        down1 = jnp.where(group_of == nz - 1, lower, lane_roll(upper, -GROUP))
+        return up0, up1, down0, down1
+
+    for index in range(9):
+        found = across(derived[index, planes], derived[index, planes + 1])
+        for number, value in enumerate(found):
+            derived[index, planes + 2 + number] = value
+
+    totals = collect(1, line_row, line_all, line)
+    count = pick(totals, 0)
+    mean_rhs = pick(totals, 1) / count
+
+    def setup(slot, above, below, coef, source):
+        level = {k: (coef(2 * n), coef(2 * n + 1)) for n, k in enumerate(LEVEL)}
+        base_bath = 0.5 * bath_sigma
+        neighbour = {0: slot, 1: above, -1: below}
+
+        def steep(dz):
+            start = 2 * len(LEVEL) + (0 if dz == 1 else 1 + 3 * len(STEEP))
+            entries = {}
+            for n, key in enumerate(STEEP):
+                entries[key] = tuple(coef(start + 1 + 3 * n + m) for m in range(3))
+            return coef(start), entries
+
+        slopes = {1: steep(1), -1: steep(-1)}
+
+        def fetch(dz, dy, rows):
+            number = {0: 0, 1: 1, -1: 2}[dy]
+            return tuple(derived[3 * number + m, neighbour[dz], rows] for m in range(3))
+
+        def edges(centre, rows, dx, terms, first):
+            t, i, v = centre
+            size = t.shape[0]
+
+            def by(value, factor):
+                if isinstance(factor, float) or factor.ndim == 0:
+                    return value * factor
+                return value * tiled(factor, size)
+
+            total = jnp.zeros((size, ny), jnp.float32)
+            image = total
+            keep = {0: slice(0, held), 1: slice(0, held), -1: slice(8, 8 + held)}[dx]
+            for number, (dz, dy) in enumerate(terms):
+                tn, i_n, vn = fetch(dz, dy, rows)
+                axis = (dz != 0) + (dx != 0) + (dy != 0) == 1
+                if dz == 0:
+                    k = SLOT[(0, dx, dy)][0]
+                    g_here, intra = level[k]
+                    g_there, bath = g_here, base_bath
+                else:
+                    bath, entries = slopes[dz]
+                    g_here, g_there, intra = entries[(dx, dy)]
+                if axis:
+                    ours = by(t, g_here - bath) + by(i, bath)
+                    theirs = by(tn, g_there - bath) + by(i_n, bath)
+                else:
+                    ours, theirs = by(t, g_here), by(tn, g_there)
+                weight = i_n * ours + i * theirs
+                weights[first + number, slot] = weight[keep]
+                total = total + weight
+                image = image + by(tn * (v - vn), intra)
+            return total, image
+
+        middle = slice(8, 8 + held)
+        full = fetch(0, 0, slice(0, deep))
+        centre = tuple(value[middle] for value in full)
+        total, image = edges(centre, middle, 0, TERMS_SAME, 0)
+        high = tuple(row_roll(value, 1)[8:deep] for value in full)
+        part = edges(high, slice(8, deep), 1, TERMS_SIDE, 8)
+        total = total + row_roll(part[0], -1)[0:held]
+        image = image + row_roll(part[1], -1)[0:held]
+        low = tuple(row_roll(value, -1)[0 : 8 + held] for value in full)
+        part = edges(low, slice(0, 8 + held), -1, TERMS_SIDE, 13)
+        total = total + row_roll(part[0], 1)[middle]
+        image = image + row_roll(part[1], 1)[middle]
+        tissue, inside, _ = centre
+        bounded = jnp.maximum(total, 1.0)
+        jacobi = inside / bounded
+        jac[slot] = jacobi + jacobi
+        spare[slot] = 2.0 * (inside - inside * (jacobi * total))
+        basis[0, slot] = jacobi * (inside * (source - mean_rhs) - tissue * image)
+        return (inside * bounded)[own]
+
+    def own_setup(slot, carry):
+        above = slot_of(slot + 1)
+        below = jnp.maximum(slot - 1, 0)
+        scale[slot] = setup(slot, above, below, lambda n: coefs[slot, n], fields[2, slot])
+        return carry
+
+    def far_setup(slot, carry):
+        j = slot_of(slot)
+        above = slot_of(jnp.minimum(j + 1, planes - 1))
+        below = slot_of(j - 1)
+        setup(slot, above, below, lambda n: coefs[slot, n], fields[2, slot])
+        return carry
+
+    def strip_setup(q, carry):
+        slot = planes + q
+        setup(slot, slot + 2, slot + 4, lambda n: coef_lanes[q, n], strips[2, q, 8 : 8 + held])
+        return carry
+
+    lax.fori_loop(0, nz, own_setup, 0)
+    lax.fori_loop(nz, planes, far_setup, 0)
+    lax.fori_loop(0, 2, strip_setup, 0)
+
+    def folded(value):
+        total = value[0:8]
+        for row in range(8, value.shape[0], 8):
+            total = total + value[row : row + 8]
+        return total
+
+    zero8 = jnp.zeros((8, ny), jnp.float32)
+
+    def record(step, sums):
+        square, cross, plain = (jnp.sum(value, axis=0, keepdims=True) for value in sums)
+        if step < ITERS:
+            dots[2 * step : 2 * step + 1] = square
+            dots[2 * ITERS + step : 2 * ITERS + step + 1] = plain
+        if step:
+            dots[2 * step - 1 : 2 * step] = cross
+
+    sums = [zero8, zero8, zero8]
+    for slot in range(nz):
+        value = basis[0, slot, own]
+        sums[0] = sums[0] + folded(value * value * scale[slot])
+        sums[2] = sums[2] + folded(value)
+    record(0, sums)
+
+    lane_of, group_of, inner_held = lanes_of(held)
+
+    def at(j):
+        return j if j < nz else 3 * nz - 1 - j
+
+    def advance(step, slot, up, down, near, rows):
+        same = None
+        for number, (dz, dy) in enumerate(TERMS_SAME):
+            value = near(dz, dy)
+            if value is None:
+                continue
+            term = weights[number, slot, rows] * value[rows]
+            same = term if same is None else same + term
+        for dx, first in ((1, 8), (-1, 13)):
+            part = None
+            for number, (dz, dy) in enumerate(TERMS_SIDE):
+                value = near(dz, dy)
+                if value is None:
+                    continue
+                term = weights[first + number, slot] * value[...]
+                part = term if part is None else part + term
+            same = same + row_roll(part, -dx)[rows]
+        value = basis[step - 1, slot, rows]
+        fresh = jac[slot, rows] * same + spare[slot, rows] * value
+        if step == 1:
+            fresh = 0.5 * fresh
+        else:
+            fresh = fresh - basis[step - 2, slot, rows]
+        basis[step, slot, rows] = fresh
+        return fresh, value
+
+    for step in range(1, ITERS + 1):
+        reach = ITERS - step
+        last = nz + reach
+        now = basis.at[step - 1]
+        for j in range(min(last + 1, planes)):
+            slot = at(j)
+            found = sides(now[slot], now[planes + slot // nz], slot % nz)
+            moved[0, slot], moved[1, slot] = found
+        if reach:
+            triples = []
+            for q in range(2):
+                values = [now[slot] for slot in range(q * nz, q * nz + nz)]
+                if q:
+                    values = [v for s, v in zip(range(nz, planes), values) if 3 * nz - 1 - s <= last]
+                strip = now[planes + q]
+                mixed = strip
+                for g in range(nz):
+                    slot = q * nz + g
+                    j = slot if q == 0 else 3 * nz - 1 - slot
+                    if j <= last:
+                        mixed = jnp.where(
+                            group_of == g, lane_roll(now[slot], GROUP * g + 8), mixed
+                        )
+                after = lane_roll(jnp.where(inner_held == 8, mixed, strip), -1)
+                before = lane_roll(jnp.where(inner_held == 7, mixed, strip), 1)
+                moved[0, planes + q], moved[1, planes + q] = after, before
+                triples.append((strip, after, before))
+            for number in range(3):
+                found = across(triples[0][number], triples[1][number])
+                for which, value in enumerate(found):
+                    beside[which, number] = value
+            for q in range(2):
+                slot = planes + q
+
+                def near(dz, dy):
+                    number = {0: 0, 1: 1, -1: 2}[dy]
+                    if dz:
+                        return beside.at[q if dz == 1 else 2 + q, number]
+                    return now.at[slot] if dy == 0 else moved.at[number - 1, slot]
+
+                advance(step, slot, None, None, near, slice(0, held))
+        sums = [zero8, zero8, zero8]
+        for j in range(last):
+            slot = at(j)
+
+            def near(dz, dy):
+                if j + dz < 0:
+                    return None
+                spot = at(j + dz)
+                return now.at[spot] if dy == 0 else moved.at[0 if dy == 1 else 1, spot]
+
+            rows = slice(0, held) if reach else own
+            fresh, value = advance(step, slot, None, None, near, rows)
+            if j < nz:
+                if reach:
+                    fresh, value = fresh[own], value[own]
+                weighted = fresh * scale[slot]
+                sums[0] = sums[0] + folded(weighted * fresh)
+                sums[1] = sums[1] + folded(weighted * value)
+                sums[2] = sums[2] + folded(fresh)
+        record(step, sums)
+
+    partial = jnp.sum(dots[...], axis=1, keepdims=True)
+    diagonal = lax.broadcasted_iota(jnp.int32, (3 * ITERS, ny), 0) == lax.broadcasted_iota(
+        jnp.int32, (3 * ITERS, ny), 1
+    )
+    final_row[...] = jnp.sum(jnp.where(diagonal, partial, 0.0), axis=0, keepdims=True)
+    spread(2, final_row, final_all, everyone)
+    for _, sends, copy in moves:
+        pl.when(sends)(copy.wait_send)
+    for copy in swaps[1:]:
+        copy.wait_send()
+    sums = collect(2, final_row, final_all, everyone)
+
+    mu = [pick(sums, n) for n in range(2 * ITERS)]
+    ones = [pick(sums, 2 * ITERS + n) for n in range(ITERS)]
+    for n in range(2, 2 * ITERS):
+        mu[n] = 2.0 * mu[n] - mu[n % 2]
+    one = jnp.ones((1, 1), jnp.float32)
+    y, p = [one], [one]
+    m_y, m_p = list(mu), list(mu)
+    x = []
+    rz = mu[0]
+
+    def plus(first, second):
+        if first is None or second is None:
+            return second if first is None else first
+        return first + second
+
+    def get(values, n):
+        return values[n] if 0 <= n < len(values) else None
+
+    for step in range(ITERS):
+        h_p = []
+        for n in range(step + 2):
+            right = get(p, n - 1)
+            if n == 1:
+                right = right + right
+            around_n = plus(get(p, n + 1), right)
+            here = get(p, n)
+            drop = None if around_n is None else -0.5 * around_n
+            h_p.append(plus(here, drop))
+        m_h = [m_p[0] - m_p[1]]
+        for n in range(1, 2 * ITERS - 1 - step):
+            m_h.append(m_p[n] - 0.5 * (m_p[n + 1] + m_p[n - 1]))
+        bottom = p[0] * m_h[0]
+        for n in range(1, step + 1):
+            bottom = bottom + p[n] * m_h[n]
+        alpha = rz / bottom
+        x = [plus(get(x, n), alpha * p[n]) for n in range(step + 1)]
+        y = [plus(get(y, n), -(alpha * h_p[n])) for n in range(step + 2)]
+        if step + 1 < ITERS:
+            m_y = [m_y[n] - alpha * m_h[n] for n in range(len(m_h))]
+            rz_next = y[0] * m_y[0]
+            for n in range(1, step + 2):
+                rz_next = rz_next + y[n] * m_y[n]
+            beta = rz_next / rz
+            p = [plus(y[n], None if n > step else beta * p[n]) for n in range(step + 2)]
+            m_p = [m_y[n] + beta * m_p[n] for n in range(len(m_y))]
+            rz = rz_next
+    mean = x[0] * ones[0]
+    for n in range(1, ITERS):
+        mean = mean + x[n] * ones[n]
+    mean = mean / count
+    xs = [jnp.broadcast_to(value, (8, ny)) for value in x]
+    ys = [jnp.broadcast_to(value, (8, ny)) for value in y]
+    mean = jnp.broadcast_to(mean, (8, ny))
+    for slot in range(nz):
+        target = flip(slot, side)
+        for row in range(0, nx, 8):
+            spot = slice(8 + row, 16 + row)
+            weight = scale[slot, row : row + 8]
+            total = jnp.where(weight > 0.0, -mean, 0.0)
+            rest = ys[ITERS] * basis[ITERS, slot, spot]
+            for n in range(ITERS):
+                value = basis[n, slot, spot]
+                total = total + xs[n] * value
+                rest = rest + ys[n] * value
+            phi[target, row : row + 8] = total
+            residual[target, row : row + 8] = weight * rest
+
+
+def fast_body(potential, tissue_mask, layer_index, source):
+    extent = tissue_mask.shape
+    nz, nx, ny = extent
+    sizes = tuple(lax.axis_size(axis) for axis in AXES)
+    planes, held, deep = 2 * nz, nx + 16, nx + 32
+    peers = math.prod(sizes)
+    vmem = pl.BlockSpec(memory_space=pltpu.VMEM)
+    hbm = pl.BlockSpec(memory_space=pltpu.HBM)
+
+    def real(*shape):
+        return pltpu.VMEM(shape + (ny,), jnp.float32)
+
+    moves = 16
+    scratch = [
+        real(3, planes, held), pltpu.VMEM(extent, jnp.int32), real(5, nx), real(2, 2, nz),
+        real(2, 2, 2, nz), real(5, deep), real(5, deep), real(5, 2, deep),
+        real(9, planes + 6, deep), real(18, planes + 2, held), real(ITERS + 1, planes + 2, held),
+        real(2, planes + 2, held), real(4, 3, held), real(planes + 2, held),
+        real(planes + 2, held), real(nz, nx), real(2, COEFS, 8), real(3 * ITERS),
+        real(1), real(sizes[1] * sizes[2], 1), real(1), real(sizes[0], 1), real(1), real(peers, 1),
+        pltpu.SMEM((LAYERS, 18), jnp.float32), pltpu.SMEM((planes, COEFS), jnp.float32),
+        pltpu.SMEM((nz,), jnp.int32), pltpu.SMEM((nz,), jnp.int32), pltpu.SMEM((planes,), jnp.int32),
+        pltpu.SemaphoreType.DMA((4,)), pltpu.SemaphoreType.DMA((moves,)),
+        pltpu.SemaphoreType.DMA((moves,)), pltpu.SemaphoreType.DMA((3,)),
+        pltpu.SemaphoreType.DMA((3,)),
+    ]
+    return tuple(
+        pl.pallas_call(
+            functools.partial(fast_kernel, extent, sizes),
+            out_shape=(jax.ShapeDtypeStruct(extent, jnp.float32),) * 2,
+            in_specs=[hbm] * 4,
+            out_specs=(vmem, vmem),
+            scratch_shapes=scratch,
+            compiler_params=pltpu.CompilerParams(
+                vmem_limit_bytes=32 * 1024 * 1024, collective_id=0, has_side_effects=True
+            ),
+        )(potential, tissue_mask, layer_index, source)
+    )
+
+
+def body(potential, tissue_mask, layer_index, source):
+    nz, nx, ny = tissue_mask.shape
+    fits = (
+        lax.axis_size("gz") == 2 and nz == 8 and ITERS == 8 and nx % 8 == 0 and nx >= 16
+        and ny == nz * GROUP and lax.axis_size("gx") > 1 and lax.axis_size("gy") > 1
+    )
+    return (fast_body if fits else general_body)(potential, tissue_mask, layer_index, source)
 
 
 def solution(mesh):

time: 68.4 us -> 40.7 us (0.60)
  Pallas kernels: 60.6 us -> 35.2 us
  other arithmetic: 3.19 us -> 0 us
  local copies, waits for them, and re-layouts: 2.87 us -> 4.61 us
    pallas_call x1, Pallas kernels: 60.6 us -> 35.2 us  [fast_body(): pl.pallas_call(functools.partial(fast_kernel, extent, sizes), out_shape=(...]
    unnamed x6 -> x10, local copies, waits for them, and re-layouts: 2.8 us -> 4.61 us
    convert_element_type x2 -> x0, other arithmetic: 1.56 us -> none  [the longest x1 1.54 us: body(): labels = tissue_mask.astype(jnp.float32)]
    concatenate x2 -> x0, other arithmetic: 0.77 us -> none  [the longest x1 0.69 us: body(): table = jnp.concatenate([table, link], axis=1)]
  transfers between devices with their start and end apart: 1 -> 0, of which waited for: 0 -> 0; matrix products, arithmetic and copies ran while one was open for 4% -> 0% of each run, Pallas kernels for 0% -> 0%
where the time goes in v1:
time: 40.7 us; the launch traced here: 40.5 us
  Pallas kernels  35.2 us (86%)
  local copies, waits for them, and re-layouts  4.61 us (11%)
  between operations  0.65 us (2%)
    pallas_call x1, Pallas kernels, fast_body(): pl.pallas_call(functools.partial(fast_kernel, extent, sizes), out_shape=(...  35.2 us
    unnamed x10, local copies, waits for them, and re-layouts  4.61 us

profile of v1, /device:TPU:0, one launch (start us, length us, event | category | flops | bytes accessed | tf_op | source)
XLA Modules:
  0.0 40.5 jit_solution(8081104295773661810)
XLA Ops:
  0.6 0.0 copy-start
  0.6 0.9 %copy-done = f32[8,24,128]{2,1,0:T(8,128)S(1)} copy-done((f32[8,24,128]{2,1,0:T(8,128)S(1)}, f32[8,24,128]{2,1,0:T(8,128)}, u32[]{:S(2)}) %copy-start) | copy-done | bytes 98328
  1.5 0.0 copy-start.1
  1.5 0.9 %copy-done.1 = s32[8,24,128]{2,1,0:T(8,128)S(1)} copy-done((s32[8,24,128]{2,1,0:T(8,128)S(1)}, s32[8,24,128]{2,1,0:T(8,128)}, u32[]{:S(2)}) %copy-start.1) | copy-done | bytes 98328
  2.4 0.0 copy-start.2
  2.4 0.9 %copy-done.2 = f32[8,24,128]{2,1,0:T(8,128)S(1)} copy-done((f32[8,24,128]{2,1,0:T(8,128)S(1)}, f32[8,24,128]{2,1,0:T(8,128)}, u32[]{:S(2)}) %copy-start.2) | copy-done | bytes 98328
  3.3 0.0 copy-start.3
  3.3 0.7 %copy-done.3 = s32[8]{0:T(128)S(1)} copy-done((s32[8]{0:T(128)S(1)}, s32[8]{0:T(128)}, u32[]{:S(2)}) %copy-start.3) | copy-done | bytes 56
  4.0 35.2 %shard_map.59 = (f32[8,24,128]{2,1,0:T(8,128)S(1)}, f32[8,24,128]{2,1,0:T(8,128)S(1)}) custom-call(f32[8,24,128]{2,1,0:T(8,128)S(1)} %copy-done, s32[8,24,128]{2,1,0:T(8,128)S(1)} %copy-done.1, s32[8]{0:T(128)S(1)} %copy-done.3, f32[8,24,128]{2,1,0:T(8,128)S(1)} %copy-done.2), custom_call_target="tpu_custom_call" | custom-call | tf_op jit(solution)/shard_map/pallas_call | solution.py:1105
  39.2 0.6 %copy.8 = f32[8,24,128]{2,1,0:T(8,128)} copy(f32[8,24,128]{2,1,0:T(8,128)S(1)} %get-tuple-element.4) | data formatting | bytes 196608
  39.9 0.6 %copy.9 = f32[8,24,128]{2,1,0:T(8,128)} copy(f32[8,24,128]{2,1,0:T(8,128)S(1)} %get-tuple-element.5) | data formatting | bytes 196608
Async XLA Ops:
  0.6 0.9 %copy-start = (f32[8,24,128]{2,1,0:T(8,128)S(1)}, f32[8,24,128]{2,1,0:T(8,128)}, u32[]{:S(2)}) copy-start(f32[8,24,128]{2,1,0:T(8,128)} %potential_in.1) | copy-start | bytes 294916
  1.5 0.9 %copy-start.1 = (s32[8,24,128]{2,1,0:T(8,128)S(1)}, s32[8,24,128]{2,1,0:T(8,128)}, u32[]{:S(2)}) copy-start(s32[8,24,128]{2,1,0:T(8,128)} %mask_in.1) | copy-start | bytes 294916
  2.4 0.9 %copy-start.2 = (f32[8,24,128]{2,1,0:T(8,128)S(1)}, f32[8,24,128]{2,1,0:T(8,128)}, u32[]{:S(2)}) copy-start(f32[8,24,128]{2,1,0:T(8,128)} %source_in.1) | copy-start | bytes 294916
  3.3 0.7 %copy-start.3 = (s32[8]{0:T(128)S(1)}, s32[8]{0:T(128)}, u32[]{:S(2)}) copy-start(s32[8]{0:T(128)} %layers_in.1) | copy-start | bytes 100

commit v2 on v1

--- a/solution.py
+++ b/solution.py
@@ -518,20 +518,6 @@
     def flip(slot, turned):
         return slot + turned * (nz - 1 - 2 * slot)
 
-    barrier = pltpu.get_barrier_semaphore()
-
-    def greet(target):
-        pl.semaphore_signal(
-            barrier, inc=1, device_id=target, device_id_type=pl.DeviceIdType.MESH
-        )
-
-    expected = len(slab) + len(line) - 2
-    for step in slab[1:] + line[1:]:
-        greet(around(*step))
-    for dx, dy in corners:
-        pl.when(exists(dx, dy))(lambda: greet((gx + dx, gy + dy, side)))
-        expected = expected + jnp.where(exists(dx, dy), 1, 0)
-
     get_layers = pltpu.make_async_copy(layers_in, layers_own, loads.at[0])
     get_mask = pltpu.make_async_copy(mask_in, labels, loads.at[1])
     get_layers.start()
@@ -544,6 +530,20 @@
             ).start()
         whole.append(pltpu.make_async_copy(ref, fields.at[index, 0:nz, own], loads.at[1 + index]))
 
+    barrier = pltpu.get_barrier_semaphore()
+
+    def greet(target):
+        pl.semaphore_signal(
+            barrier, inc=1, device_id=target, device_id_type=pl.DeviceIdType.MESH
+        )
+
+    expected = len(slab) + len(line) - 2
+    for step in slab[1:] + line[1:]:
+        greet(around(*step))
+    for dx, dy in corners:
+        pl.when(exists(dx, dy))(lambda: greet((gx + dx, gy + dy, side)))
+        expected = expected + jnp.where(exists(dx, dy), 1, 0)
+
     def clear(when, ref, index):
         @pl.when(when)
         def _():
@@ -552,16 +552,13 @@
     every = slice(None)
     clear(first_x, fields, (every, slice(0, nz), slice(0, 8)))
     clear(last_x, fields, (every, slice(0, nz), slice(8 + nx, held)))
-    clear(first_x, edge_recv, (0, 0))
-    clear(last_x, edge_recv, (0, 1))
+    for index in range(2):
+        clear(first_x, edge_recv, (0, index, 0))
+        clear(last_x, edge_recv, (0, index, 1))
     for ref, edge in ((from_after, last_y), (from_before, first_y)):
         clear(edge, ref, (every,))
         clear(first_x, ref, (every, slice(0, 16)))
         clear(last_x, ref, (every, slice(16 + nx, deep)))
-    for layer in range(LAYERS):
-        for column in range(18):
-            table[layer, column] = jnp.float32(HALF_TABLE[layer, column])
-
     def lanes_of(rows):
         lane = lax.broadcasted_iota(jnp.int32, (rows, ny), 1)
         return lane, lane // GROUP, lane % GROUP
@@ -573,6 +570,11 @@
     for copy in whole:
         copy.wait()
 
+    lane = lax.broadcasted_iota(jnp.int32, (1, ny), 1)
+
+    def pick(vector, index):
+        return jnp.sum(jnp.where(lane == index, vector, 0.0), axis=1, keepdims=True)
+
     _, group, inner = lanes_of(nx)
 
     def packed(values, shift):
@@ -584,70 +586,12 @@
 
     for index in range(3):
         values = [fields[index, slot, own] for slot in range(nz)]
-        packs[index] = packed(values, 8)
+        packs[2 * index] = packed(values, 8)
         if index < 2:
-            packs[3 + index] = jnp.where(inner == 15, packed(values, 7), packed(values, 9))
+            packs[2 * index + 1] = jnp.where(inner == 15, packed(values, 7), packed(values, 9))
             for slot in range(nz):
-                edge_send[0, index, slot : slot + 1] = values[slot][8:9]
-                edge_send[1, index, slot : slot + 1] = values[slot][nx - 9 : nx - 8]
-
-    pl.semaphore_wait(barrier, expected)
-
-    def link(number, src, dst, target):
-        return pltpu.make_async_remote_copy(
-            src_ref=src, dst_ref=dst, send_sem=halo_send.at[number],
-            recv_sem=halo_recv.at[number], device_id=target,
-            device_id_type=pl.DeviceIdType.MESH,
-        )
-
-    moves = []
-
-    def move(dx, dy, src, dst):
-        copy = link(len(moves), src, dst, (gx + dx, gy + dy, side))
-        pl.when(exists(dx, dy))(copy.start)
-        moves.append((exists(-dx, -dy), exists(dx, dy), copy))
-
-    for dx, dy in corners:
-        into = from_before if dy == 1 else from_after
-        if dx == 1:
-            move(dx, dy, packs.at[:, nx - 16 : nx], into.at[:, 0:16])
-        else:
-            move(dx, dy, packs.at[:, 0:16], into.at[:, 16 + nx : deep])
-    move(0, 1, packs, from_before.at[:, 16 : 16 + nx])
-    move(0, -1, packs, from_after.at[:, 16 : 16 + nx])
-    move(1, 0, edge_send.at[1], edge_recv.at[0, 0])
-    move(-1, 0, edge_send.at[0], edge_recv.at[0, 1])
-    move(1, 0, fields.at[:, 0:nz, nx : nx + 8], fields.at[:, 0:nz, 0:8])
-    move(-1, 0, fields.at[:, 0:nz, 8:16], fields.at[:, 0:nz, 8 + nx : held])
-    other = (gx, gy, 1 - side)
-    base = len(moves)
-    swaps = [
-        link(base, layers_own, layers_far, other),
-        link(base + 1, fields.at[:, 0:nz, own], fields.at[:, nz:planes, own], other),
-    ]
-    for copy in swaps:
-        copy.start()
-
-    def spread(number, row, gathered, targets):
-        for index, step in enumerate(targets):
-            if index:
-                pltpu.make_async_remote_copy(
-                    src_ref=row, dst_ref=gathered.at[index], send_sem=sum_send.at[number],
-                    recv_sem=sum_recv.at[number], device_id=around(*step),
-                    device_id_type=pl.DeviceIdType.MESH,
-                ).start()
-
-    def collect(number, row, gathered, targets):
-        arrived = gathered.at[pl.ds(1, len(targets) - 1)]
-        pltpu.make_async_copy(arrived, arrived, sum_recv.at[number]).wait()
-        pltpu.make_async_copy(arrived, arrived, sum_send.at[number]).wait()
-        gathered[0] = row[...]
-        return jnp.sum(gathered[...], axis=0)
-
-    lane = lax.broadcasted_iota(jnp.int32, (1, ny), 1)
-
-    def pick(vector, index):
-        return jnp.sum(jnp.where(lane == index, vector, 0.0), axis=1, keepdims=True)
+                edge_send[index, 0, slot : slot + 1] = values[slot][8:9]
+                edge_send[index, 1, slot : slot + 1] = values[slot][nx - 9 : nx - 8]
 
     cells = jnp.zeros((8, ny), jnp.float32)
     injected = cells
@@ -659,9 +603,88 @@
     cells = jnp.sum(jnp.sum(cells, axis=0, keepdims=True), axis=1, keepdims=True)
     injected = jnp.sum(jnp.sum(injected, axis=0, keepdims=True), axis=1, keepdims=True)
     early_row[...] = jnp.where(lane == 0, cells, jnp.where(lane == 1, injected, 0.0))
+
+    pl.semaphore_wait(barrier, expected)
+
+    def spread(number, row, gathered, targets):
+        for index, step in enumerate(targets):
+            if index:
+                pltpu.make_async_remote_copy(
+                    src_ref=row, dst_ref=gathered.at[index], send_sem=sum_send.at[number],
+                    recv_sem=sum_recv.at[number], device_id=around(*step),
+                    device_id_type=pl.DeviceIdType.MESH,
+                ).start()
+
+    def collect(number, row, gathered, targets):
+        arrived = gathered.at[pl.ds(1, len(targets) - 1)]
+        pltpu.make_async_copy(arrived, arrived, sum_recv.at[number]).wait()
+        pltpu.make_async_copy(arrived, arrived, sum_send.at[number]).wait()
+        gathered[0] = row[...]
+        return jnp.sum(gathered[...], axis=0)
+
     spread(0, early_row, early_all, slab)
 
-    swaps[0].wait()
+    def link(number, src, dst, target):
+        return pltpu.make_async_remote_copy(
+            src_ref=src, dst_ref=dst, send_sem=halo_send.at[number],
+            recv_sem=halo_recv.at[number], device_id=target,
+            device_id_type=pl.DeviceIdType.MESH,
+        )
+
+    other = (gx, gy, 1 - side)
+    numbers = iter(range(64))
+
+    def swap(src, dst):
+        copy = link(next(numbers), src, dst, other)
+        copy.start()
+        return copy
+
+    def exchange(picked, rows, edge):
+        found = []
+
+        def move(dx, dy, src, dst):
+            copy = link(next(numbers), src, dst, (gx + dx, gy + dy, side))
+            pl.when(exists(dx, dy))(copy.start)
+            found.append((exists(-dx, -dy), exists(dx, dy), copy))
+
+        for dx, dy in corners:
+            into = from_before if dy == 1 else from_after
+            if dx == 1:
+                move(dx, dy, packs.at[picked, nx - 16 : nx], into.at[picked, 0:16])
+            else:
+                move(dx, dy, packs.at[picked, 0:16], into.at[picked, 16 + nx : deep])
+        move(0, 1, packs.at[picked], from_before.at[picked, 16 : 16 + nx])
+        move(0, -1, packs.at[picked], from_after.at[picked, 16 : 16 + nx])
+        move(1, 0, edge_send.at[edge, 1], edge_recv.at[0, edge, 0])
+        move(-1, 0, edge_send.at[edge, 0], edge_recv.at[0, edge, 1])
+        move(1, 0, fields.at[rows, 0:nz, nx : nx + 8], fields.at[rows, 0:nz, 0:8])
+        move(-1, 0, fields.at[rows, 0:nz, 8:16], fields.at[rows, 0:nz, 8 + nx : held])
+        return found
+
+    groups = [(slice(0, 2), slice(0, 1), 0), (slice(2, 5), slice(1, 3), 1)]
+    layer_swap = swap(layers_own, layers_far)
+    moves, relays = [], []
+    for picked, rows, edge in groups:
+        moves.append(exchange(picked, rows, edge))
+        relays.append([swap(fields.at[rows, 0:nz, own], fields.at[rows, nz:planes, own])])
+
+    def relay(picked, rows, edge):
+        for receives, _, copy in moves[edge]:
+            pl.when(receives)(copy.wait_recv)
+        for index in range(picked.start, picked.stop):
+            strips[index, 0] = jnp.where(inner_deep < 8, from_before[index], from_after[index])
+        relays[edge] += [
+            swap(strips.at[picked, 0], strips.at[picked, 1]),
+            swap(edge_recv.at[0, edge], edge_recv.at[1, edge]),
+            swap(fields.at[rows, 0:nz, 0:8], fields.at[rows, nz:planes, 0:8]),
+            swap(fields.at[rows, 0:nz, 8 + nx : held], fields.at[rows, nz:planes, 8 + nx : held]),
+        ]
+
+    for layer in range(LAYERS):
+        for column in range(18):
+            table[layer, column] = jnp.float32(HALF_TABLE[layer, column])
+
+    layer_swap.wait()
     for slot in range(nz):
         layers[slot] = layers_own[flip(slot, side)]
         layers[nz + slot] = layers_far[flip(slot, 1 - side)]
@@ -701,25 +724,10 @@
 
     lax.fori_loop(0, COEFS, widen, 0)
 
+    lane_of, group_of, inner_deep = lanes_of(deep)
+    relay(*groups[0])
     line_row[...] = collect(0, early_row, early_all, slab)
     spread(1, line_row, line_all, line)
-
-    for receives, _, copy in moves:
-        pl.when(receives)(copy.wait_recv)
-    _, _, inner_deep = lanes_of(deep)
-    for index in range(5):
-        strips[index, 0] = jnp.where(inner_deep < 8, from_before[index], from_after[index])
-    late = [
-        (strips.at[:, 0], strips.at[:, 1]),
-        (edge_recv.at[0], edge_recv.at[1]),
-        (fields.at[:, 0:nz, 0:8], fields.at[:, nz:planes, 0:8]),
-        (fields.at[:, 0:nz, 8 + nx : held], fields.at[:, nz:planes, 8 + nx : held]),
-    ]
-    for number, (src, dst) in enumerate(late):
-        swaps.append(link(base + 2 + number, src, dst, other))
-        swaps[-1].start()
-
-    lane_deep, group_deep, inner_deep = lanes_of(deep)
 
     def sides(value, strip, g):
         ring = lane_roll(strip, -(GROUP * g + 8))
@@ -727,48 +735,44 @@
         before = lane_roll(jnp.where(lane_of == ny - 1, ring, value), 1)
         return after, before
 
-    def inserted(values):
-        total = lane_roll(values[0], 8)
-        for g in range(1, len(values)):
-            total = jnp.where(group_of == g, lane_roll(values[g], GROUP * g + 8), total)
-        return total
-
-    def stored(number, slot, label, volts):
-        derived[3 * number, slot] = jnp.where(label == 2.0, 1.0, 0.0)
-        derived[3 * number + 1, slot] = jnp.where(label > 0.0, 1.0, 0.0)
-        derived[3 * number + 2, slot] = volts
-
-    lane_of, group_of = lane_deep, group_deep
+    def stored(index, number, slot, value):
+        if index:
+            derived[3 * number + 2, slot] = value
+        else:
+            derived[3 * number, slot] = jnp.where(value == 2.0, 1.0, 0.0)
+            derived[3 * number + 1, slot] = jnp.where(value > 0.0, 1.0, 0.0)
 
     def framed_plane(index, q, g):
-        before = jnp.broadcast_to(edge_recv[q, 0, index, g : g + 1], (8, ny))
-        after = jnp.broadcast_to(edge_recv[q, 1, index, g : g + 1], (8, ny))
+        before = jnp.broadcast_to(edge_recv[q, index, 0, g : g + 1], (8, ny))
+        after = jnp.broadcast_to(edge_recv[q, index, 1, g : g + 1], (8, ny))
         return jnp.concatenate([before, fields[index, q * nz + g], after], axis=0)
 
-    for q in range(2):
-        if q:
-            for copy in swaps[1:]:
-                copy.wait_recv()
-        found = [[], []]
-        for g in range(nz):
-            parts = []
-            for index in range(2):
+    def derive(index):
+        def one(q, carry):
+            @pl.when(q == 1)
+            def _():
+                for copy in relays[index]:
+                    copy.wait_recv()
+
+            strip, edge = strips[2 * index, q], strips[2 * index + 1, q]
+            mixed = strip
+            for g in range(nz):
                 value = framed_plane(index, q, g)
-                found[index].append(value)
-                parts.append((value,) + sides(value, strips[index, q], g))
-            for number in range(3):
-                stored(number, q * nz + g, parts[0][number], parts[1][number])
-        parts = []
-        for index in range(2):
-            value, edge = strips[index, q], strips[3 + index, q]
-            mixed = inserted(found[index])
-            after = lane_roll(jnp.where(inner_deep == 8, mixed, value), -1)
-            before = lane_roll(jnp.where(inner_deep == 7, mixed, value), 1)
-            after = jnp.where(inner_deep == 15, edge, after)
-            before = jnp.where(inner_deep == 0, edge, before)
-            parts.append((value, after, before))
-        for number in range(3):
-            stored(number, planes + q, parts[0][number], parts[1][number])
+                mixed = jnp.where(group_of == g, lane_roll(value, GROUP * g + 8), mixed)
+                for number, part in enumerate((value,) + sides(value, strip, g)):
+                    stored(index, number, q * nz + g, part)
+            after = lane_roll(jnp.where(inner_deep == 8, mixed, strip), -1)
+            before = lane_roll(jnp.where(inner_deep == 7, mixed, strip), 1)
+            stored(index, 0, planes + q, strip)
+            stored(index, 1, planes + q, jnp.where(inner_deep == 15, edge, after))
+            stored(index, 2, planes + q, jnp.where(inner_deep == 0, edge, before))
+            return carry
+
+        lax.fori_loop(0, 2, one, 0)
+        for number in ((2, 5, 8) if index else (0, 1, 3, 4, 6, 7)):
+            found = across(derived[number, planes], derived[number, planes + 1])
+            for shift, value in enumerate(found):
+                derived[number, planes + 2 + shift] = value
 
     def across(lower, upper):
         up0 = jnp.where(group_of == nz - 1, upper, lane_roll(lower, -GROUP))
@@ -777,107 +781,143 @@
         down1 = jnp.where(group_of == nz - 1, lower, lane_roll(upper, -GROUP))
         return up0, up1, down0, down1
 
-    for index in range(9):
-        found = across(derived[index, planes], derived[index, planes + 1])
-        for number, value in enumerate(found):
-            derived[index, planes + 2 + number] = value
-
-    totals = collect(1, line_row, line_all, line)
-    count = pick(totals, 0)
-    mean_rhs = pick(totals, 1) / count
-
-    def setup(slot, above, below, coef, source):
-        level = {k: (coef(2 * n), coef(2 * n + 1)) for n, k in enumerate(LEVEL)}
+    derive(0)
+
+    def level_of(coef):
+        return {k: (coef(2 * n), coef(2 * n + 1)) for n, k in enumerate(LEVEL)}
+
+    def steep_of(coef, dz):
+        start = 2 * len(LEVEL) + (0 if dz == 1 else 1 + 3 * len(STEEP))
+        entries = {}
+        for n, key in enumerate(STEEP):
+            entries[key] = tuple(coef(start + 1 + 3 * n + m) for m in range(3))
+        return coef(start), entries
+
+    middle = slice(8, 8 + held)
+
+    def by(value, factor):
+        if isinstance(factor, float) or factor.ndim == 0:
+            return value * factor
+        return value * tiled(factor, value.shape[0])
+
+    def gathered_terms(edges, full):
+        sums = edges(tuple(value[middle] for value in full), middle, 0, TERMS_SAME, 0)
+        high = tuple(row_roll(value, 1)[8:deep] for value in full)
+        part = edges(high, slice(8, deep), 1, TERMS_SIDE, 8)
+        sums = sums + row_roll(part, -1)[0:held]
+        low = tuple(row_roll(value, -1)[0 : 8 + held] for value in full)
+        part = edges(low, slice(0, 8 + held), -1, TERMS_SIDE, 13)
+        return sums + row_roll(part, 1)[middle]
+
+    def weigh(slot, above, below, coef):
+        level, slopes = level_of(coef), {1: steep_of(coef, 1), -1: steep_of(coef, -1)}
         base_bath = 0.5 * bath_sigma
         neighbour = {0: slot, 1: above, -1: below}
 
-        def steep(dz):
-            start = 2 * len(LEVEL) + (0 if dz == 1 else 1 + 3 * len(STEEP))
-            entries = {}
-            for n, key in enumerate(STEEP):
-                entries[key] = tuple(coef(start + 1 + 3 * n + m) for m in range(3))
-            return coef(start), entries
-
-        slopes = {1: steep(1), -1: steep(-1)}
-
         def fetch(dz, dy, rows):
             number = {0: 0, 1: 1, -1: 2}[dy]
-            return tuple(derived[3 * number + m, neighbour[dz], rows] for m in range(3))
+            return tuple(derived[3 * number + m, neighbour[dz], rows] for m in range(2))
 
         def edges(centre, rows, dx, terms, first):
-            t, i, v = centre
-            size = t.shape[0]
-
-            def by(value, factor):
-                if isinstance(factor, float) or factor.ndim == 0:
-                    return value * factor
-                return value * tiled(factor, size)
-
-            total = jnp.zeros((size, ny), jnp.float32)
-            image = total
+            t, i = centre
+            total = None
             keep = {0: slice(0, held), 1: slice(0, held), -1: slice(8, 8 + held)}[dx]
             for number, (dz, dy) in enumerate(terms):
-                tn, i_n, vn = fetch(dz, dy, rows)
-                axis = (dz != 0) + (dx != 0) + (dy != 0) == 1
+                tn, i_n = fetch(dz, dy, rows)
                 if dz == 0:
-                    k = SLOT[(0, dx, dy)][0]
-                    g_here, intra = level[k]
-                    g_there, bath = g_here, base_bath
+                    g_here = g_there = level[SLOT[(0, dx, dy)][0]][0]
+                    bath = base_bath
                 else:
                     bath, entries = slopes[dz]
-                    g_here, g_there, intra = entries[(dx, dy)]
-                if axis:
+                    g_here, g_there, _ = entries[(dx, dy)]
+                if (dz != 0) + (dx != 0) + (dy != 0) == 1:
                     ours = by(t, g_here - bath) + by(i, bath)
                     theirs = by(tn, g_there - bath) + by(i_n, bath)
                 else:
                     ours, theirs = by(t, g_here), by(tn, g_there)
                 weight = i_n * ours + i * theirs
                 weights[first + number, slot] = weight[keep]
-                total = total + weight
-                image = image + by(tn * (v - vn), intra)
-            return total, image
-
-        middle = slice(8, 8 + held)
+                total = weight if total is None else total + weight
+            return total
+
         full = fetch(0, 0, slice(0, deep))
-        centre = tuple(value[middle] for value in full)
-        total, image = edges(centre, middle, 0, TERMS_SAME, 0)
-        high = tuple(row_roll(value, 1)[8:deep] for value in full)
-        part = edges(high, slice(8, deep), 1, TERMS_SIDE, 8)
-        total = total + row_roll(part[0], -1)[0:held]
-        image = image + row_roll(part[1], -1)[0:held]
-        low = tuple(row_roll(value, -1)[0 : 8 + held] for value in full)
-        part = edges(low, slice(0, 8 + held), -1, TERMS_SIDE, 13)
-        total = total + row_roll(part[0], 1)[middle]
-        image = image + row_roll(part[1], 1)[middle]
-        tissue, inside, _ = centre
+        total = gathered_terms(edges, full)
+        inside = full[1][middle]
         bounded = jnp.maximum(total, 1.0)
         jacobi = inside / bounded
         jac[slot] = jacobi + jacobi
         spare[slot] = 2.0 * (inside - inside * (jacobi * total))
-        basis[0, slot] = jacobi * (inside * (source - mean_rhs) - tissue * image)
         return (inside * bounded)[own]
 
-    def own_setup(slot, carry):
-        above = slot_of(slot + 1)
-        below = jnp.maximum(slot - 1, 0)
-        scale[slot] = setup(slot, above, below, lambda n: coefs[slot, n], fields[2, slot])
-        return carry
-
-    def far_setup(slot, carry):
+    def begin(slot, above, below, coef, source):
+        level, slopes = level_of(coef), {1: steep_of(coef, 1), -1: steep_of(coef, -1)}
+        neighbour = {0: slot, 1: above, -1: below}
+
+        def edges(centre, rows, dx, terms, first):
+            v = centre[0]
+            image = None
+            for dz, dy in terms:
+                number = {0: 0, 1: 1, -1: 2}[dy]
+                tn = derived[3 * number, neighbour[dz], rows]
+                vn = derived[3 * number + 2, neighbour[dz], rows]
+                if dz == 0:
+                    intra = level[SLOT[(0, dx, dy)][0]][1]
+                else:
+                    intra = slopes[dz][1][(dx, dy)][2]
+                term = by(tn * (v - vn), intra)
+                image = term if image is None else image + term
+            return image
+
+        image = gathered_terms(edges, (derived[2, slot],))
+        tissue, inside = derived[0, slot, middle], derived[1, slot, middle]
+        value = 0.5 * jac[slot] * (inside * (source - mean_rhs) - tissue * image)
+        basis[0, slot] = value
+        return value[own]
+
+    def beyond(slot):
         j = slot_of(slot)
-        above = slot_of(jnp.minimum(j + 1, planes - 1))
-        below = slot_of(j - 1)
-        setup(slot, above, below, lambda n: coefs[slot, n], fields[2, slot])
-        return carry
-
-    def strip_setup(q, carry):
+        return slot_of(jnp.minimum(j + 1, planes - 1)), slot_of(jnp.maximum(j - 1, 0))
+
+    def from_table(slot):
+        return lambda n: coefs[slot, n]
+
+    def from_lanes(q):
+        return lambda n: coef_lanes[q, n]
+
+    def own_weigh(slot, carry):
+        scale[slot] = weigh(slot, *beyond(slot), from_table(slot))
+        return carry
+
+    def far_weigh(slot, carry):
+        weigh(slot, *beyond(slot), from_table(slot))
+        return carry
+
+    def strip_weigh(q, carry):
         slot = planes + q
-        setup(slot, slot + 2, slot + 4, lambda n: coef_lanes[q, n], strips[2, q, 8 : 8 + held])
-        return carry
-
-    lax.fori_loop(0, nz, own_setup, 0)
-    lax.fori_loop(nz, planes, far_setup, 0)
-    lax.fori_loop(0, 2, strip_setup, 0)
+        weigh(slot, slot + 2, slot + 4, from_lanes(q))
+        return carry
+
+    lax.fori_loop(0, nz, own_weigh, 0)
+    relay(*groups[1])
+    lax.fori_loop(nz, planes, far_weigh, 0)
+    lax.fori_loop(0, 2, strip_weigh, 0)
+    derive(1)
+
+    totals = collect(1, line_row, line_all, line)
+    count = pick(totals, 0)
+    mean_rhs = pick(totals, 1) / count
+
+    def plane_begin(slot, carry):
+        begin(slot, *beyond(slot), from_table(slot), fields[2, slot])
+        return carry
+
+    def strip_begin(q, carry):
+        slot = planes + q
+        begin(slot, slot + 2, slot + 4, from_lanes(q), strips[4, q, middle])
+        return carry
+
+    lax.fori_loop(0, planes, plane_begin, 0)
+    lax.fori_loop(0, 2, strip_begin, 0)
 
     def folded(value):
         total = value[0:8]
@@ -888,12 +928,8 @@
     zero8 = jnp.zeros((8, ny), jnp.float32)
 
     def record(step, sums):
-        square, cross, plain = (jnp.sum(value, axis=0, keepdims=True) for value in sums)
-        if step < ITERS:
-            dots[2 * step : 2 * step + 1] = square
-            dots[2 * ITERS + step : 2 * ITERS + step + 1] = plain
-        if step:
-            dots[2 * step - 1 : 2 * step] = cross
+        for kind, value in enumerate(sums):
+            dots[kind * (ITERS + 1) + step] = value
 
     sums = [zero8, zero8, zero8]
     for slot in range(nz):
@@ -907,7 +943,7 @@
     def at(j):
         return j if j < nz else 3 * nz - 1 - j
 
-    def advance(step, slot, up, down, near, rows):
+    def advance(step, slot, near, rows, first):
         same = None
         for number, (dz, dy) in enumerate(TERMS_SAME):
             value = near(dz, dy)
@@ -915,38 +951,35 @@
                 continue
             term = weights[number, slot, rows] * value[rows]
             same = term if same is None else same + term
-        for dx, first in ((1, 8), (-1, 13)):
+        for dx, begin in ((1, 8), (-1, 13)):
             part = None
             for number, (dz, dy) in enumerate(TERMS_SIDE):
                 value = near(dz, dy)
                 if value is None:
                     continue
-                term = weights[first + number, slot] * value[...]
+                term = weights[begin + number, slot] * value[...]
                 part = term if part is None else part + term
             same = same + row_roll(part, -dx)[rows]
         value = basis[step - 1, slot, rows]
         fresh = jac[slot, rows] * same + spare[slot, rows] * value
-        if step == 1:
-            fresh = 0.5 * fresh
+        if first:
+            factor = jnp.where(step == 1, 0.5, 1.0).astype(jnp.float32)
+            back = jnp.where(step == 1, 0.0, 1.0).astype(jnp.float32)
+            fresh = factor * fresh - back * basis[jnp.maximum(step - 2, 0), slot, rows]
         else:
             fresh = fresh - basis[step - 2, slot, rows]
         basis[step, slot, rows] = fresh
         return fresh, value
 
-    for step in range(1, ITERS + 1):
-        reach = ITERS - step
-        last = nz + reach
+    def one_step(step, last, first=False, final=False):
         now = basis.at[step - 1]
         for j in range(min(last + 1, planes)):
             slot = at(j)
             found = sides(now[slot], now[planes + slot // nz], slot % nz)
             moved[0, slot], moved[1, slot] = found
-        if reach:
+        if not final:
             triples = []
             for q in range(2):
-                values = [now[slot] for slot in range(q * nz, q * nz + nz)]
-                if q:
-                    values = [v for s, v in zip(range(nz, planes), values) if 3 * nz - 1 - s <= last]
                 strip = now[planes + q]
                 mixed = strip
                 for g in range(nz):
@@ -973,7 +1006,7 @@
                         return beside.at[q if dz == 1 else 2 + q, number]
                     return now.at[slot] if dy == 0 else moved.at[number - 1, slot]
 
-                advance(step, slot, None, None, near, slice(0, held))
+                advance(step, slot, near, slice(0, held), first)
         sums = [zero8, zero8, zero8]
         for j in range(last):
             slot = at(j)
@@ -984,10 +1017,10 @@
                 spot = at(j + dz)
                 return now.at[spot] if dy == 0 else moved.at[0 if dy == 1 else 1, spot]
 
-            rows = slice(0, held) if reach else own
-            fresh, value = advance(step, slot, None, None, near, rows)
+            rows = own if final else slice(0, held)
+            fresh, value = advance(step, slot, near, rows, first)
             if j < nz:
-                if reach:
+                if not final:
                     fresh, value = fresh[own], value[own]
                 weighted = fresh * scale[slot]
                 sums[0] = sums[0] + folded(weighted * fresh)
@@ -995,20 +1028,34 @@
                 sums[2] = sums[2] + folded(fresh)
         record(step, sums)
 
-    partial = jnp.sum(dots[...], axis=1, keepdims=True)
-    diagonal = lax.broadcasted_iota(jnp.int32, (3 * ITERS, ny), 0) == lax.broadcasted_iota(
-        jnp.int32, (3 * ITERS, ny), 1
-    )
-    final_row[...] = jnp.sum(jnp.where(diagonal, partial, 0.0), axis=0, keepdims=True)
+    def early_steps(step, carry):
+        one_step(step, planes - 1, first=True)
+        return carry
+
+    def later_steps(step, carry):
+        one_step(step, planes - 4)
+        return carry
+
+    lax.fori_loop(1, 4, early_steps, 0)
+    lax.fori_loop(4, ITERS, later_steps, 0)
+    one_step(ITERS, nz, final=True)
+    partial = jnp.sum(jnp.sum(dots[...], axis=1), axis=1, keepdims=True)
+    entry = lax.broadcasted_iota(jnp.int32, (3 * (ITERS + 1), ny), 0)
+    kind, index = entry // (ITERS + 1), entry % (ITERS + 1)
+    place_of = jnp.where(kind == 0, 2 * index, jnp.where(kind == 1, 2 * index - 1, 2 * ITERS + 1 + index))
+    wanted = place_of == lax.broadcasted_iota(jnp.int32, entry.shape, 1)
+    final_row[...] = jnp.sum(jnp.where(wanted, partial, 0.0), axis=0, keepdims=True)
     spread(2, final_row, final_all, everyone)
-    for _, sends, copy in moves:
-        pl.when(sends)(copy.wait_send)
-    for copy in swaps[1:]:
-        copy.wait_send()
+    for group in moves:
+        for _, sends, copy in group:
+            pl.when(sends)(copy.wait_send)
+    for group in relays:
+        for copy in group:
+            copy.wait_send()
     sums = collect(2, final_row, final_all, everyone)
 
     mu = [pick(sums, n) for n in range(2 * ITERS)]
-    ones = [pick(sums, 2 * ITERS + n) for n in range(ITERS)]
+    ones = [pick(sums, 2 * ITERS + 1 + n) for n in range(ITERS)]
     for n in range(2, 2 * ITERS):
         mu[n] = 2.0 * mu[n] - mu[n % 2]
     one = jnp.ones((1, 1), jnp.float32)
@@ -1087,13 +1134,14 @@
     def real(*shape):
         return pltpu.VMEM(shape + (ny,), jnp.float32)
 
-    moves = 16
+    moves = 40
+    inputs = (potential, tissue_mask, layer_index, source)
     scratch = [
         real(3, planes, held), pltpu.VMEM(extent, jnp.int32), real(5, nx), real(2, 2, nz),
         real(2, 2, 2, nz), real(5, deep), real(5, deep), real(5, 2, deep),
         real(9, planes + 6, deep), real(18, planes + 2, held), real(ITERS + 1, planes + 2, held),
         real(2, planes + 2, held), real(4, 3, held), real(planes + 2, held),
-        real(planes + 2, held), real(nz, nx), real(2, COEFS, 8), real(3 * ITERS),
+        real(planes + 2, held), real(nz, nx), real(2, COEFS, 8), real(3 * (ITERS + 1), 8),
         real(1), real(sizes[1] * sizes[2], 1), real(1), real(sizes[0], 1), real(1), real(peers, 1),
         pltpu.SMEM((LAYERS, 18), jnp.float32), pltpu.SMEM((planes, COEFS), jnp.float32),
         pltpu.SMEM((nz,), jnp.int32), pltpu.SMEM((nz,), jnp.int32), pltpu.SMEM((planes,), jnp.int32),
@@ -1111,7 +1159,7 @@
             compiler_params=pltpu.CompilerParams(
                 vmem_limit_bytes=32 * 1024 * 1024, collective_id=0, has_side_effects=True
             ),
-        )(potential, tissue_mask, layer_index, source)
+        )(*(pltpu.with_memory_space_constraint(ref, pltpu.HBM) for ref in inputs))
     )
 
 

time: 40.7 us -> 32.8 us (0.81)
  Pallas kernels: 35.2 us -> 30.7 us
  local copies, waits for them, and re-layouts: 4.61 us -> 1.28 us
    pallas_call x1, Pallas kernels: 35.2 us -> 30.7 us  [fast_body(): pl.pallas_call(functools.partial(fast_kernel, extent, sizes), out_shape=(...]
    unnamed x10 -> x2, local copies, waits for them, and re-layouts: 4.61 us -> 1.28 us
where the time goes in v2:
time: 32.8 us; the launch traced here: 32.6 us
  Pallas kernels  30.7 us (94%)
  local copies, waits for them, and re-layouts  1.28 us (4%)
  between operations  0.64 us (2%)
    pallas_call x1, Pallas kernels, fast_body(): pl.pallas_call(functools.partial(fast_kernel, extent, sizes), out_shape=(...  30.7 us
    unnamed x2, local copies, waits for them, and re-layouts  1.28 us

profile of v2, /device:TPU:0, one launch (start us, length us, event | category | flops | bytes accessed | tf_op | source)
XLA Modules:
  0.0 32.6 jit_solution(17124254697171365085)
XLA Ops:
  0.6 30.7 %shard_map.59 = (f32[8,24,128]{2,1,0:T(8,128)S(1)}, f32[8,24,128]{2,1,0:T(8,128)S(1)}) custom-call(f32[8,24,128]{2,1,0:T(8,128)} %potential_in.1, s32[8,24,128]{2,1,0:T(8,128)} %mask_in.1, s32[8]{0:T(128)} %layers_in.1, f32[8,24,128]{2,1,0:T(8,128)} %source_in.1), custom_call_target="tpu_custom_call" | custom-call | tf_op jit(solution)/shard_map/pallas_call | solution.py:1153
  31.3 0.6 %copy.8 = f32[8,24,128]{2,1,0:T(8,128)} copy(f32[8,24,128]{2,1,0:T(8,128)S(1)} %get-tuple-element.4) | data formatting | bytes 196608
  32.0 0.6 %copy.9 = f32[8,24,128]{2,1,0:T(8,128)} copy(f32[8,24,128]{2,1,0:T(8,128)S(1)} %get-tuple-element.5) | data formatting | bytes 196608

commit v3 on v2

--- a/solution.py
+++ b/solution.py
@@ -446,7 +446,8 @@
 TERMS_SIDE = [(0, 0), (0, 1), (0, -1), (1, 0), (-1, 0)]
 LEVEL = [0, 1, 3, 4]
 STEEP = [(0, 0), (1, 0), (-1, 0), (0, 1), (0, -1)]
-COEFS = 2 * len(LEVEL) + 2 * (1 + 3 * len(STEEP))
+UPWARD = 2 * len(LEVEL)
+COEFS = UPWARD + 1 + 3 * len(STEEP)
 
 
 def numpy_table(longitudinal, transverse):
@@ -563,36 +564,115 @@
         lane = lax.broadcasted_iota(jnp.int32, (rows, ny), 1)
         return lane, lane // GROUP, lane % GROUP
 
-    get_layers.wait()
-    get_mask.wait()
-    for plane in range(nz):
-        fields[0, flip(plane, side), own] = labels[plane].astype(jnp.float32)
-    for copy in whole:
-        copy.wait()
-
     lane = lax.broadcasted_iota(jnp.int32, (1, ny), 1)
 
     def pick(vector, index):
         return jnp.sum(jnp.where(lane == index, vector, 0.0), axis=1, keepdims=True)
 
-    _, group, inner = lanes_of(nx)
-
-    def packed(values, shift):
-        total = values[0]
-        total = lane_roll(total, shift)
-        for g in range(1, nz):
-            total = jnp.where(group == g, lane_roll(values[g], GROUP * g + shift), total)
-        return total
-
-    for index in range(3):
+    own_lane, _, _ = lanes_of(nx)
+    later = (own_lane + 1) % ny // GROUP
+    sooner = (own_lane + ny - 1) % ny // GROUP
+
+    def pack(index):
         values = [fields[index, slot, own] for slot in range(nz)]
-        packs[2 * index] = packed(values, 8)
+        turned = [lane_roll(value, GROUP * slot + 8) for slot, value in enumerate(values)]
+        for toward, owner in ((0, later), (1, sooner)):
+            total = turned[0]
+            for slot in range(1, nz):
+                total = jnp.where(owner == slot, turned[slot], total)
+            packs[index, toward] = total
         if index < 2:
-            packs[2 * index + 1] = jnp.where(inner == 15, packed(values, 7), packed(values, 9))
             for slot in range(nz):
                 edge_send[index, 0, slot : slot + 1] = values[slot][8:9]
                 edge_send[index, 1, slot : slot + 1] = values[slot][nx - 9 : nx - 8]
 
+    def spread(number, row, gathered, targets):
+        for index, step in enumerate(targets):
+            if index:
+                pltpu.make_async_remote_copy(
+                    src_ref=row, dst_ref=gathered.at[index], send_sem=sum_send.at[number],
+                    recv_sem=sum_recv.at[number], device_id=around(*step),
+                    device_id_type=pl.DeviceIdType.MESH,
+                ).start()
+
+    def collect(number, row, gathered, targets):
+        arrived = gathered.at[pl.ds(1, len(targets) - 1)]
+        pltpu.make_async_copy(arrived, arrived, sum_recv.at[number]).wait()
+        pltpu.make_async_copy(arrived, arrived, sum_send.at[number]).wait()
+        gathered[0] = row[...]
+        return jnp.sum(gathered[...], axis=0)
+
+    def link(number, src, dst, target):
+        return pltpu.make_async_remote_copy(
+            src_ref=src, dst_ref=dst, send_sem=halo_send.at[number],
+            recv_sem=halo_recv.at[number], device_id=target,
+            device_id_type=pl.DeviceIdType.MESH,
+        )
+
+    other = (gx, gy, 1 - side)
+    numbers = iter(range(64))
+
+    def swap(src, dst):
+        copy = link(next(numbers), src, dst, other)
+        copy.start()
+        return copy
+
+    def exchange(picked, rows, edge):
+        found = []
+
+        def move(dx, dy, src, dst):
+            copy = link(next(numbers), src, dst, (gx + dx, gy + dy, side))
+            pl.when(exists(dx, dy))(copy.start)
+            found.append((exists(-dx, -dy), exists(dx, dy), copy))
+
+        for dx, dy in corners:
+            into, toward = (from_before, 0) if dy == 1 else (from_after, 1)
+            if dx == 1:
+                move(dx, dy, packs.at[rows, toward, nx - 16 : nx], into.at[rows, 0:16])
+            else:
+                move(dx, dy, packs.at[rows, toward, 0:16], into.at[rows, 16 + nx : deep])
+        move(0, 1, packs.at[rows, 0], from_before.at[rows, 16 : 16 + nx])
+        move(0, -1, packs.at[rows, 1], from_after.at[rows, 16 : 16 + nx])
+        move(1, 0, edge_send.at[edge, 1], edge_recv.at[0, edge, 0])
+        move(-1, 0, edge_send.at[edge, 0], edge_recv.at[0, edge, 1])
+        move(1, 0, fields.at[rows, 0:nz, nx : nx + 8], fields.at[rows, 0:nz, 0:8])
+        move(-1, 0, fields.at[rows, 0:nz, 8:16], fields.at[rows, 0:nz, 8 + nx : held])
+        return found
+
+    groups = [(slice(0, 2), slice(0, 1), 0), (slice(2, 5), slice(1, 3), 1)]
+    moves, relays = [], []
+
+    def launch(picked, rows, edge):
+        moves.append(exchange(picked, rows, edge))
+        relays.append([swap(fields.at[rows, 0:nz, own], fields.at[rows, nz:planes, own])])
+
+    def relay(picked, rows, edge):
+        for receives, _, copy in moves[edge]:
+            pl.when(receives)(copy.wait_recv)
+        for index in range(rows.start, rows.stop):
+            below, above = from_before[index], from_after[index]
+            strips[2 * index, 0] = jnp.where(inner_deep < 8, below, above)
+            if index < 2:
+                strips[2 * index + 1, 0] = jnp.where(
+                    inner_deep == 15, lane_roll(above, -1), lane_roll(below, 1)
+                )
+        relays[edge] += [
+            swap(strips.at[picked, 0], strips.at[picked, 1]),
+            swap(edge_recv.at[0, edge], edge_recv.at[1, edge]),
+            swap(fields.at[rows, 0:nz, 0:8], fields.at[rows, nz:planes, 0:8]),
+            swap(fields.at[rows, 0:nz, 8 + nx : held], fields.at[rows, nz:planes, 8 + nx : held]),
+        ]
+
+    get_mask.wait()
+    get_layers.wait()
+    for plane in range(nz):
+        fields[0, flip(plane, side), own] = labels[plane].astype(jnp.float32)
+    pack(0)
+    pl.semaphore_wait(barrier, expected)
+    layer_swap = swap(layers_own, layers_far)
+    launch(*groups[0])
+    for copy in whole:
+        copy.wait()
     cells = jnp.zeros((8, ny), jnp.float32)
     injected = cells
     for slot in range(nz):
@@ -604,81 +684,9 @@
     injected = jnp.sum(jnp.sum(injected, axis=0, keepdims=True), axis=1, keepdims=True)
     early_row[...] = jnp.where(lane == 0, cells, jnp.where(lane == 1, injected, 0.0))
 
-    pl.semaphore_wait(barrier, expected)
-
-    def spread(number, row, gathered, targets):
-        for index, step in enumerate(targets):
-            if index:
-                pltpu.make_async_remote_copy(
-                    src_ref=row, dst_ref=gathered.at[index], send_sem=sum_send.at[number],
-                    recv_sem=sum_recv.at[number], device_id=around(*step),
-                    device_id_type=pl.DeviceIdType.MESH,
-                ).start()
-
-    def collect(number, row, gathered, targets):
-        arrived = gathered.at[pl.ds(1, len(targets) - 1)]
-        pltpu.make_async_copy(arrived, arrived, sum_recv.at[number]).wait()
-        pltpu.make_async_copy(arrived, arrived, sum_send.at[number]).wait()
-        gathered[0] = row[...]
-        return jnp.sum(gathered[...], axis=0)
-
     spread(0, early_row, early_all, slab)
-
-    def link(number, src, dst, target):
-        return pltpu.make_async_remote_copy(
-            src_ref=src, dst_ref=dst, send_sem=halo_send.at[number],
-            recv_sem=halo_recv.at[number], device_id=target,
-            device_id_type=pl.DeviceIdType.MESH,
-        )
-
-    other = (gx, gy, 1 - side)
-    numbers = iter(range(64))
-
-    def swap(src, dst):
-        copy = link(next(numbers), src, dst, other)
-        copy.start()
-        return copy
-
-    def exchange(picked, rows, edge):
-        found = []
-
-        def move(dx, dy, src, dst):
-            copy = link(next(numbers), src, dst, (gx + dx, gy + dy, side))
-            pl.when(exists(dx, dy))(copy.start)
-            found.append((exists(-dx, -dy), exists(dx, dy), copy))
-
-        for dx, dy in corners:
-            into = from_before if dy == 1 else from_after
-            if dx == 1:
-                move(dx, dy, packs.at[picked, nx - 16 : nx], into.at[picked, 0:16])
-            else:
-                move(dx, dy, packs.at[picked, 0:16], into.at[picked, 16 + nx : deep])
-        move(0, 1, packs.at[picked], from_before.at[picked, 16 : 16 + nx])
-        move(0, -1, packs.at[picked], from_after.at[picked, 16 : 16 + nx])
-        move(1, 0, edge_send.at[edge, 1], edge_recv.at[0, edge, 0])
-        move(-1, 0, edge_send.at[edge, 0], edge_recv.at[0, edge, 1])
-        move(1, 0, fields.at[rows, 0:nz, nx : nx + 8], fields.at[rows, 0:nz, 0:8])
-        move(-1, 0, fields.at[rows, 0:nz, 8:16], fields.at[rows, 0:nz, 8 + nx : held])
-        return found
-
-    groups = [(slice(0, 2), slice(0, 1), 0), (slice(2, 5), slice(1, 3), 1)]
-    layer_swap = swap(layers_own, layers_far)
-    moves, relays = [], []
-    for picked, rows, edge in groups:
-        moves.append(exchange(picked, rows, edge))
-        relays.append([swap(fields.at[rows, 0:nz, own], fields.at[rows, nz:planes, own])])
-
-    def relay(picked, rows, edge):
-        for receives, _, copy in moves[edge]:
-            pl.when(receives)(copy.wait_recv)
-        for index in range(picked.start, picked.stop):
-            strips[index, 0] = jnp.where(inner_deep < 8, from_before[index], from_after[index])
-        relays[edge] += [
-            swap(strips.at[picked, 0], strips.at[picked, 1]),
-            swap(edge_recv.at[0, edge], edge_recv.at[1, edge]),
-            swap(fields.at[rows, 0:nz, 0:8], fields.at[rows, nz:planes, 0:8]),
-            swap(fields.at[rows, 0:nz, 8 + nx : held], fields.at[rows, nz:planes, 8 + nx : held]),
-        ]
+    pack(1)
+    pack(2)
 
     for layer in range(LAYERS):
         for column in range(18):
@@ -692,43 +700,52 @@
     def slot_of(j):
         return jnp.where(j < nz, j, 3 * nz - 1 - j)
 
-    def coefficients(slot, carry):
-        j = slot_of(slot)
-        layer = layers[slot]
-        for n, k in enumerate(LEVEL):
-            coefs[slot, 2 * n] = table[layer, k]
-            coefs[slot, 2 * n + 1] = 2.0 * table[layer, 9 + k]
-        for half, dz in enumerate((1, -1)):
-            near = (j + dz >= 0) & (j + dz < planes)
-            there = layers[slot_of(jnp.where(near, j + dz, j))]
+    def coefficients(pair, carry):
+        for slot in (2 * pair, 2 * pair + 1):
+            j = slot_of(slot)
+            layer = layers[slot]
+            for n, k in enumerate(LEVEL):
+                coefs[slot, 2 * n] = table[layer, k]
+                coefs[slot, 2 * n + 1] = 2.0 * table[layer, 9 + k]
+            near = j + 1 < planes
+            there = layers[slot_of(jnp.where(near, j + 1, j))]
             open_ = jnp.where(near, 1.0, 0.0).astype(jnp.float32)
-            start = 2 * len(LEVEL) + half * (1 + 3 * len(STEEP))
-            coefs[slot, start] = 0.5 * bath_sigma * open_
+            coefs[slot, UPWARD] = 0.5 * bath_sigma * open_
             for n, (dx, dy) in enumerate(STEEP):
-                k = column_of(dz, dx, dy, side)
-                coefs[slot, start + 1 + 3 * n] = table[layer, k] * open_
-                coefs[slot, start + 2 + 3 * n] = table[there, k] * open_
-                coefs[slot, start + 3 + 3 * n] = (table[layer, 9 + k] + table[there, 9 + k]) * open_
-        return carry
-
-    lax.fori_loop(0, planes, coefficients, 0)
+                k = column_of(1, dx, dy, side)
+                coefs[slot, UPWARD + 1 + 3 * n] = table[layer, k] * open_
+                coefs[slot, UPWARD + 2 + 3 * n] = table[there, k] * open_
+                coefs[slot, UPWARD + 3 + 3 * n] = (table[layer, 9 + k] + table[there, 9 + k]) * open_
+        return carry
+
+    launch(*groups[1])
+    lax.fori_loop(0, nz, coefficients, 0)
+    for n in range(COEFS):
+        coefs[planes, n] = jnp.float32(0.0)
     _, group8, _ = lanes_of(8)
 
-    def widen(n, carry):
-        for q in range(2):
-            value = jnp.full((8, ny), coefs[q * nz, n], jnp.float32)
-            for g in range(1, nz):
-                value = jnp.where(group8 == g, coefs[q * nz + g, n], value)
-            coef_lanes[q, n] = value
-        return carry
-
-    lax.fori_loop(0, COEFS, widen, 0)
+    def at(j):
+        return j if j < nz else 3 * nz - 1 - j
+
+    def widen(block, carry):
+        for n in [8 * block + m for m in range(8)]:
+            for q in range(2):
+                for which, shift in enumerate((0, -1)):
+                    value = None
+                    for g in range(nz):
+                        j = at(q * nz + g) + shift
+                        entry = coefs[planes if j < 0 else at(j), n]
+                        if value is None:
+                            value = jnp.full((8, ny), entry, jnp.float32)
+                        else:
+                            value = jnp.where(group8 == g, entry, value)
+                    coef_lanes[which, q, n] = value
+        return carry
+
+    lax.fori_loop(0, COEFS // 8, widen, 0)
 
     lane_of, group_of, inner_deep = lanes_of(deep)
     relay(*groups[0])
-    line_row[...] = collect(0, early_row, early_all, slab)
-    spread(1, line_row, line_all, line)
-
     def sides(value, strip, g):
         ring = lane_roll(strip, -(GROUP * g + 8))
         after = lane_roll(jnp.where(lane_of == 0, ring, value), -1)
@@ -747,28 +764,21 @@
         after = jnp.broadcast_to(edge_recv[q, index, 1, g : g + 1], (8, ny))
         return jnp.concatenate([before, fields[index, q * nz + g], after], axis=0)
 
-    def derive(index):
-        def one(q, carry):
-            @pl.when(q == 1)
-            def _():
-                for copy in relays[index]:
-                    copy.wait_recv()
-
-            strip, edge = strips[2 * index, q], strips[2 * index + 1, q]
-            mixed = strip
-            for g in range(nz):
-                value = framed_plane(index, q, g)
-                mixed = jnp.where(group_of == g, lane_roll(value, GROUP * g + 8), mixed)
-                for number, part in enumerate((value,) + sides(value, strip, g)):
-                    stored(index, number, q * nz + g, part)
-            after = lane_roll(jnp.where(inner_deep == 8, mixed, strip), -1)
-            before = lane_roll(jnp.where(inner_deep == 7, mixed, strip), 1)
-            stored(index, 0, planes + q, strip)
-            stored(index, 1, planes + q, jnp.where(inner_deep == 15, edge, after))
-            stored(index, 2, planes + q, jnp.where(inner_deep == 0, edge, before))
-            return carry
-
-        lax.fori_loop(0, 2, one, 0)
+    def derive(index, q):
+        strip, edge = strips[2 * index, q], strips[2 * index + 1, q]
+        mixed = strip
+        for g in range(nz):
+            value = framed_plane(index, q, g)
+            mixed = jnp.where(group_of == g, lane_roll(value, GROUP * g + 8), mixed)
+            for number, part in enumerate((value,) + sides(value, strip, g)):
+                stored(index, number, q * nz + g, part)
+        after = lane_roll(jnp.where(inner_deep == 8, mixed, strip), -1)
+        before = lane_roll(jnp.where(inner_deep == 7, mixed, strip), 1)
+        stored(index, 0, planes + q, strip)
+        stored(index, 1, planes + q, jnp.where(inner_deep == 15, edge, after))
+        stored(index, 2, planes + q, jnp.where(inner_deep == 0, edge, before))
+
+    def derive_beside(index):
         for number in ((2, 5, 8) if index else (0, 1, 3, 4, 6, 7)):
             found = across(derived[number, planes], derived[number, planes + 1])
             for shift, value in enumerate(found):
@@ -781,17 +791,18 @@
         down1 = jnp.where(group_of == nz - 1, lower, lane_roll(upper, -GROUP))
         return up0, up1, down0, down1
 
-    derive(0)
-
     def level_of(coef):
-        return {k: (coef(2 * n), coef(2 * n + 1)) for n, k in enumerate(LEVEL)}
+        return {k: (coef(1, 2 * n), coef(1, 2 * n + 1)) for n, k in enumerate(LEVEL)}
 
     def steep_of(coef, dz):
-        start = 2 * len(LEVEL) + (0 if dz == 1 else 1 + 3 * len(STEEP))
         entries = {}
-        for n, key in enumerate(STEEP):
-            entries[key] = tuple(coef(start + 1 + 3 * n + m) for m in range(3))
-        return coef(start), entries
+        for n, (dx, dy) in enumerate(STEEP):
+            here, there, intra = (coef(dz, UPWARD + 1 + 3 * n + m) for m in range(3))
+            if dz == 1:
+                entries[(dx, dy)] = here, there, intra
+            else:
+                entries[(-dx, -dy)] = there, here, intra
+        return coef(dz, UPWARD), entries
 
     middle = slice(8, 8 + held)
 
@@ -879,17 +890,15 @@
         return slot_of(jnp.minimum(j + 1, planes - 1)), slot_of(jnp.maximum(j - 1, 0))
 
     def from_table(slot):
-        return lambda n: coefs[slot, n]
+        j = slot_of(slot)
+        under = jnp.where(j == 0, planes, slot_of(j - 1))
+        return lambda dz, n: coefs[slot if dz == 1 else under, n]
 
     def from_lanes(q):
-        return lambda n: coef_lanes[q, n]
-
-    def own_weigh(slot, carry):
+        return lambda dz, n: coef_lanes[0 if dz == 1 else 1, q, n]
+
+    def plane_weigh(slot, carry):
         scale[slot] = weigh(slot, *beyond(slot), from_table(slot))
-        return carry
-
-    def far_weigh(slot, carry):
-        weigh(slot, *beyond(slot), from_table(slot))
         return carry
 
     def strip_weigh(q, carry):
@@ -897,11 +906,34 @@
         weigh(slot, slot + 2, slot + 4, from_lanes(q))
         return carry
 
-    lax.fori_loop(0, nz, own_weigh, 0)
+    def label_half(q, carry):
+        @pl.when(q == 1)
+        def _():
+            for copy in relays[0]:
+                copy.wait_recv()
+            line_row[...] = collect(0, early_row, early_all, slab)
+            spread(1, line_row, line_all, line)
+
+        derive(0, q)
+        lax.fori_loop(q * (nz - 1), nz - 1 + q, plane_weigh, 0)
+        return carry
+
+    lax.fori_loop(0, 2, label_half, 0)
     relay(*groups[1])
-    lax.fori_loop(nz, planes, far_weigh, 0)
+    lax.fori_loop(nz, planes, plane_weigh, 0)
+    derive_beside(0)
     lax.fori_loop(0, 2, strip_weigh, 0)
-    derive(1)
+    def volt_half(q, carry):
+        @pl.when(q == 1)
+        def _():
+            for copy in relays[1]:
+                copy.wait_recv()
+
+        derive(1, q)
+        return carry
+
+    lax.fori_loop(0, 2, volt_half, 0)
+    derive_beside(1)
 
     totals = collect(1, line_row, line_all, line)
     count = pick(totals, 0)
@@ -939,9 +971,6 @@
     record(0, sums)
 
     lane_of, group_of, inner_held = lanes_of(held)
-
-    def at(j):
-        return j if j < nz else 3 * nz - 1 - j
 
     def advance(step, slot, near, rows, first):
         same = None
@@ -1137,13 +1166,13 @@
     moves = 40
     inputs = (potential, tissue_mask, layer_index, source)
     scratch = [
-        real(3, planes, held), pltpu.VMEM(extent, jnp.int32), real(5, nx), real(2, 2, nz),
-        real(2, 2, 2, nz), real(5, deep), real(5, deep), real(5, 2, deep),
+        real(3, planes, held), pltpu.VMEM(extent, jnp.int32), real(3, 2, nx), real(2, 2, nz),
+        real(2, 2, 2, nz), real(3, deep), real(3, deep), real(5, 2, deep),
         real(9, planes + 6, deep), real(18, planes + 2, held), real(ITERS + 1, planes + 2, held),
         real(2, planes + 2, held), real(4, 3, held), real(planes + 2, held),
-        real(planes + 2, held), real(nz, nx), real(2, COEFS, 8), real(3 * (ITERS + 1), 8),
+        real(planes + 2, held), real(planes, nx), real(2, 2, COEFS, 8), real(3 * (ITERS + 1), 8),
         real(1), real(sizes[1] * sizes[2], 1), real(1), real(sizes[0], 1), real(1), real(peers, 1),
-        pltpu.SMEM((LAYERS, 18), jnp.float32), pltpu.SMEM((planes, COEFS), jnp.float32),
+        pltpu.SMEM((LAYERS, 18), jnp.float32), pltpu.SMEM((planes + 1, COEFS), jnp.float32),
         pltpu.SMEM((nz,), jnp.int32), pltpu.SMEM((nz,), jnp.int32), pltpu.SMEM((planes,), jnp.int32),
         pltpu.SemaphoreType.DMA((4,)), pltpu.SemaphoreType.DMA((moves,)),
         pltpu.SemaphoreType.DMA((moves,)), pltpu.SemaphoreType.DMA((3,)),

time: 32.8 us -> 30.2 us (0.921)
  Pallas kernels: 30.7 us -> 28.1 us
    pallas_call x1, Pallas kernels: 30.7 us -> 28.1 us  [fast_body(): pl.pallas_call(functools.partial(fast_kernel, extent, sizes), out_shape=(...]
where the time goes in v3:
time: 30.2 us; the launch traced here: 30.1 us
  Pallas kernels  28.1 us (93%)
  local copies, waits for them, and re-layouts  1.28 us (4%)
  between operations  0.64 us (2%)
    pallas_call x1, Pallas kernels, fast_body(): pl.pallas_call(functools.partial(fast_kernel, extent, sizes), out_shape=(...  28.1 us
    unnamed x2, local copies, waits for them, and re-layouts  1.28 us

profile of v3, /device:TPU:0, one launch (start us, length us, event | category | flops | bytes accessed | tf_op | source)
XLA Modules:
  0.0 30.1 jit_solution(15979015107894105773)
XLA Ops:
  0.6 28.1 %shard_map.59 = (f32[8,24,128]{2,1,0:T(8,128)S(1)}, f32[8,24,128]{2,1,0:T(8,128)S(1)}) custom-call(f32[8,24,128]{2,1,0:T(8,128)} %potential_in.1, s32[8,24,128]{2,1,0:T(8,128)} %mask_in.1, s32[8]{0:T(128)} %layers_in.1, f32[8,24,128]{2,1,0:T(8,128)} %source_in.1), custom_call_target="tpu_custom_call" | custom-call | tf_op jit(solution)/shard_map/pallas_call | solution.py:1182
  28.8 0.6 %copy.8 = f32[8,24,128]{2,1,0:T(8,128)} copy(f32[8,24,128]{2,1,0:T(8,128)S(1)} %get-tuple-element.4) | data formatting | bytes 196608
  29.4 0.6 %copy.9 = f32[8,24,128]{2,1,0:T(8,128)} copy(f32[8,24,128]{2,1,0:T(8,128)S(1)} %get-tuple-element.5) | data formatting | bytes 196608

commit v4 on v3

--- a/solution.py
+++ b/solution.py
@@ -472,7 +472,8 @@
 
 
 def lane_roll(value, step):
-    return pltpu.roll(value, step % value.shape[1], 1)
+    size = value.shape[1]
+    return pltpu.roll(value, step % size if isinstance(step, int) else lax.rem(step + size, size), 1)
 
 
 def row_roll(value, step):
@@ -746,8 +747,10 @@
 
     lane_of, group_of, inner_deep = lanes_of(deep)
     relay(*groups[0])
-    def sides(value, strip, g):
-        ring = lane_roll(strip, -(GROUP * g + 8))
+    def ring_of(strip, g):
+        return lane_roll(strip, -(GROUP * g + 8))
+
+    def sides(value, ring):
         after = lane_roll(jnp.where(lane_of == 0, ring, value), -1)
         before = lane_roll(jnp.where(lane_of == ny - 1, ring, value), 1)
         return after, before
@@ -760,18 +763,18 @@
             derived[3 * number + 1, slot] = jnp.where(value > 0.0, 1.0, 0.0)
 
     def framed_plane(index, q, g):
-        before = jnp.broadcast_to(edge_recv[q, index, 0, g : g + 1], (8, ny))
-        after = jnp.broadcast_to(edge_recv[q, index, 1, g : g + 1], (8, ny))
+        before = jnp.broadcast_to(edge_recv[q, index, 0, pl.ds(g, 1)], (8, ny))
+        after = jnp.broadcast_to(edge_recv[q, index, 1, pl.ds(g, 1)], (8, ny))
         return jnp.concatenate([before, fields[index, q * nz + g], after], axis=0)
 
-    def derive(index, q):
+    def derive_plane(index, q, g, mixed, ring):
+        value = framed_plane(index, q, g)
+        for number, part in enumerate((value,) + sides(value, ring)):
+            stored(index, number, q * nz + g, part)
+        return jnp.where(group_of == g, lane_roll(value, GROUP * g + 8), mixed)
+
+    def derive_strip(index, q, mixed):
         strip, edge = strips[2 * index, q], strips[2 * index + 1, q]
-        mixed = strip
-        for g in range(nz):
-            value = framed_plane(index, q, g)
-            mixed = jnp.where(group_of == g, lane_roll(value, GROUP * g + 8), mixed)
-            for number, part in enumerate((value,) + sides(value, strip, g)):
-                stored(index, number, q * nz + g, part)
         after = lane_roll(jnp.where(inner_deep == 8, mixed, strip), -1)
         before = lane_roll(jnp.where(inner_deep == 7, mixed, strip), 1)
         stored(index, 0, planes + q, strip)
@@ -914,26 +917,31 @@
             line_row[...] = collect(0, early_row, early_all, slab)
             spread(1, line_row, line_all, line)
 
-        derive(0, q)
+        mixed = strips[0, q]
+        for g in range(nz):
+            mixed = derive_plane(0, q, g, mixed, ring_of(strips[0, q], g))
+        derive_strip(0, q, mixed)
         lax.fori_loop(q * (nz - 1), nz - 1 + q, plane_weigh, 0)
         return carry
 
     lax.fori_loop(0, 2, label_half, 0)
     relay(*groups[1])
-    lax.fori_loop(nz, planes, plane_weigh, 0)
+    def derive_pair(q, pair, mixed):
+        for g in (2 * pair, 2 * pair + 1):
+            mixed = derive_plane(1, q, g, mixed, ring_of(strips[2, q], g))
+        return mixed
+
+    def far_weigh(pair, mixed):
+        for m in range(2):
+            plane_weigh(nz + 2 * pair + m, 0)
+        return derive_pair(0, pair, mixed)
+
+    mixed = lax.fori_loop(0, nz // 2, far_weigh, strips[2, 0])
+    derive_strip(1, 0, mixed)
     derive_beside(0)
     lax.fori_loop(0, 2, strip_weigh, 0)
-    def volt_half(q, carry):
-        @pl.when(q == 1)
-        def _():
-            for copy in relays[1]:
-                copy.wait_recv()
-
-        derive(1, q)
-        return carry
-
-    lax.fori_loop(0, 2, volt_half, 0)
-    derive_beside(1)
+    for copy in relays[1]:
+        copy.wait_recv()
 
     totals = collect(1, line_row, line_all, line)
     count = pick(totals, 0)
@@ -942,13 +950,21 @@
     def plane_begin(slot, carry):
         begin(slot, *beyond(slot), from_table(slot), fields[2, slot])
         return carry
+
+    def own_begin(pair, mixed):
+        plane_begin(2 * pair, 0)
+        plane_begin(jnp.minimum(2 * pair + 1, nz - 2), 0)
+        return derive_pair(1, pair, mixed)
 
     def strip_begin(q, carry):
         slot = planes + q
         begin(slot, slot + 2, slot + 4, from_lanes(q), strips[4, q, middle])
         return carry
 
-    lax.fori_loop(0, planes, plane_begin, 0)
+    mixed = lax.fori_loop(0, nz // 2, own_begin, strips[2, 1])
+    derive_strip(1, 1, mixed)
+    derive_beside(1)
+    lax.fori_loop(nz - 1, planes, plane_begin, 0)
     lax.fori_loop(0, 2, strip_begin, 0)
 
     def folded(value):
@@ -1004,7 +1020,7 @@
         now = basis.at[step - 1]
         for j in range(min(last + 1, planes)):
             slot = at(j)
-            found = sides(now[slot], now[planes + slot // nz], slot % nz)
+            found = sides(now[slot], ring_of(now[planes + slot // nz], slot % nz))
             moved[0, slot], moved[1, slot] = found
         if not final:
             triples = []
@@ -1151,6 +1167,17 @@
             residual[target, row : row + 8] = weight * rest
 
 
+def hand_out(phi, residual, phi_out, residual_out, sems):
+    copies = [
+        pltpu.make_async_copy(phi, phi_out, sems.at[0]),
+        pltpu.make_async_copy(residual, residual_out, sems.at[1]),
+    ]
+    for copy in copies:
+        copy.start()
+    for copy in copies:
+        copy.wait()
+
+
 def fast_body(potential, tissue_mask, layer_index, source):
     extent = tissue_mask.shape
     nz, nx, ny = extent
@@ -1178,17 +1205,26 @@
         pltpu.SemaphoreType.DMA((moves,)), pltpu.SemaphoreType.DMA((3,)),
         pltpu.SemaphoreType.DMA((3,)),
     ]
+    shapes = (jax.ShapeDtypeStruct(extent, jnp.float32),) * 2
+    found = pl.pallas_call(
+        functools.partial(fast_kernel, extent, sizes),
+        out_shape=shapes,
+        in_specs=[hbm] * 4,
+        out_specs=(vmem, vmem),
+        scratch_shapes=scratch,
+        compiler_params=pltpu.CompilerParams(
+            vmem_limit_bytes=32 * 1024 * 1024, collective_id=0, has_side_effects=True
+        ),
+    )(*(pltpu.with_memory_space_constraint(ref, pltpu.HBM) for ref in inputs))
     return tuple(
         pl.pallas_call(
-            functools.partial(fast_kernel, extent, sizes),
-            out_shape=(jax.ShapeDtypeStruct(extent, jnp.float32),) * 2,
-            in_specs=[hbm] * 4,
-            out_specs=(vmem, vmem),
-            scratch_shapes=scratch,
-            compiler_params=pltpu.CompilerParams(
-                vmem_limit_bytes=32 * 1024 * 1024, collective_id=0, has_side_effects=True
-            ),
-        )(*(pltpu.with_memory_space_constraint(ref, pltpu.HBM) for ref in inputs))
+            hand_out,
+            out_shape=shapes,
+            in_specs=[vmem] * 2,
+            out_specs=(hbm, hbm),
+            scratch_shapes=[pltpu.SemaphoreType.DMA((2,))],
+            compiler_params=pltpu.CompilerParams(vmem_limit_bytes=4 * 1024 * 1024),
+        )(*found)
     )
 
 

time: 30.2 us -> 29.6 us (0.980)
  local copies, waits for them, and re-layouts: 1.28 us -> 0 us
  Pallas kernels: 28.1 us -> 28.8 us
    unnamed x2 -> x0, local copies, waits for them, and re-layouts: 1.28 us -> none
    pallas_call x1 -> x2, Pallas kernels: 28.1 us -> 28.8 us  [the longest x1 28.1 us: fast_body(): pl.pallas_call(functools.partial(fast_kernel, extent, sizes), out_shape=s...]
where the time goes in v4:
time: 29.6 us; the launch traced here: 29.4 us
  Pallas kernels  28.8 us (97%)
  between operations  0.64 us (2%)
    pallas_call x1, Pallas kernels, fast_body(): pl.pallas_call(functools.partial(fast_kernel, extent, sizes), out_shape=s...  28.1 us
    pallas_call x1, Pallas kernels, fast_body(): pl.pallas_call(hand_out, out_shape=shapes, in_specs=[vmem] * 2, out_specs...  0.69 us

profile of v4, /device:TPU:0, one launch (start us, length us, event | category | flops | bytes accessed | tf_op | source)
XLA Modules:
  0.0 29.4 jit_solution(15722401851116515861)
XLA Ops:
  0.6 28.1 %shard_map.59 = (f32[8,24,128]{2,1,0:T(8,128)S(1)}, f32[8,24,128]{2,1,0:T(8,128)S(1)}) custom-call(f32[8,24,128]{2,1,0:T(8,128)} %potential_in.1, s32[8,24,128]{2,1,0:T(8,128)} %mask_in.1, s32[8]{0:T(128)} %layers_in.1, f32[8,24,128]{2,1,0:T(8,128)} %source_in.1), custom_call_target="tpu_custom_call" | custom-call | tf_op jit(solution)/shard_map/pallas_call | solution.py:1209
  28.7 0.7 %shard_map.60 = (f32[8,24,128]{2,1,0:T(8,128)}, f32[8,24,128]{2,1,0:T(8,128)}) custom-call(f32[8,24,128]{2,1,0:T(8,128)S(1)} %get-tuple-element.4.phi, f32[8,24,128]{2,1,0:T(8,128)S(1)} %get-tuple-element.5.residual), custom_call_target="tpu_custom_call" | custom-call | tf_op jit(solution)/shard_map/pallas_call | solution.py:1220

commit v5 on v4

--- a/solution.py
+++ b/solution.py
@@ -494,7 +494,7 @@
                 derived, weights, basis, moved, beside, jac, spare, scale, coef_lanes, dots,
                 early_row, early_all, line_row, line_all, final_row, final_all,
                 table, coefs, layers_own, layers_far, layers,
-                loads, halo_send, halo_recv, sum_send, sum_recv):
+                loads, halo_send, halo_recv, sum_send, sum_recv, reached):
     nz, nx, ny = extent
     planes, held, deep = 2 * nz, nx + 16, nx + 32
     own = slice(8, 8 + nx)
@@ -539,12 +539,12 @@
             barrier, inc=1, device_id=target, device_id_type=pl.DeviceIdType.MESH
         )
 
-    expected = len(slab) + len(line) - 2
-    for step in slab[1:] + line[1:]:
-        greet(around(*step))
-    for dx, dy in corners:
+    expected = len(slab) - 1
+    for dx, dy in corners + [(1, 0), (-1, 0)]:
         pl.when(exists(dx, dy))(lambda: greet((gx + dx, gy + dy, side)))
         expected = expected + jnp.where(exists(dx, dy), 1, 0)
+    for step in slab[1:]:
+        greet(around(*step))
 
     def clear(when, ref, index):
         @pl.when(when)
@@ -747,6 +747,12 @@
 
     lane_of, group_of, inner_deep = lanes_of(deep)
     relay(*groups[0])
+    for dx in (1, -1):
+        @pl.when(exists(dx, 0))
+        def _():
+            pl.semaphore_signal(
+                reached, inc=1, device_id=(gx + dx, gy, side), device_id_type=pl.DeviceIdType.MESH
+            )
     def ring_of(strip, g):
         return lane_roll(strip, -(GROUP * g + 8))
 
@@ -884,9 +890,7 @@
 
         image = gathered_terms(edges, (derived[2, slot],))
         tissue, inside = derived[0, slot, middle], derived[1, slot, middle]
-        value = 0.5 * jac[slot] * (inside * (source - mean_rhs) - tissue * image)
-        basis[0, slot] = value
-        return value[own]
+        basis[0, slot] = 0.5 * jac[slot] * (inside * source - tissue * image)
 
     def beyond(slot):
         j = slot_of(slot)
@@ -915,6 +919,8 @@
             for copy in relays[0]:
                 copy.wait_recv()
             line_row[...] = collect(0, early_row, early_all, slab)
+            sides_x = jnp.where(exists(1, 0), 1, 0) + jnp.where(exists(-1, 0), 1, 0)
+            pl.semaphore_wait(reached, sides_x)
             spread(1, line_row, line_all, line)
 
         mixed = strips[0, q]
@@ -943,10 +949,6 @@
     for copy in relays[1]:
         copy.wait_recv()
 
-    totals = collect(1, line_row, line_all, line)
-    count = pick(totals, 0)
-    mean_rhs = pick(totals, 1) / count
-
     def plane_begin(slot, carry):
         begin(slot, *beyond(slot), from_table(slot), fields[2, slot])
         return carry
@@ -979,11 +981,19 @@
         for kind, value in enumerate(sums):
             dots[kind * (ITERS + 1) + step] = value
 
+    totals = collect(1, line_row, line_all, line)
+    count = pick(totals, 0)
+    mean_rhs = pick(totals, 1) / count
+
+    half_mean = 0.5 * mean_rhs
     sums = [zero8, zero8, zero8]
-    for slot in range(nz):
-        value = basis[0, slot, own]
-        sums[0] = sums[0] + folded(value * value * scale[slot])
-        sums[2] = sums[2] + folded(value)
+    for slot in range(planes + 2):
+        value = basis[0, slot] - half_mean * jac[slot]
+        basis[0, slot] = value
+        if slot < nz:
+            value = value[own]
+            sums[0] = sums[0] + folded(value * value * scale[slot])
+            sums[2] = sums[2] + folded(value)
     record(0, sums)
 
     lane_of, group_of, inner_held = lanes_of(held)
@@ -1016,44 +1026,86 @@
         basis[step, slot, rows] = fresh
         return fresh, value
 
+    LEAD = 4
+
+    def roll_plane(field, j, ring):
+        slot = at(j)
+        moved[0, slot], moved[1, slot] = sides(field[slot], ring)
+
+    def ring_plane(field, j):
+        slot = at(j)
+        return ring_of(field[planes + slot // nz], slot % nz)
+
     def one_step(step, last, first=False, final=False):
         now = basis.at[step - 1]
-        for j in range(min(last + 1, planes)):
-            slot = at(j)
-            found = sides(now[slot], ring_of(now[planes + slot // nz], slot % nz))
-            moved[0, slot], moved[1, slot] = found
-        if not final:
-            triples = []
-            for q in range(2):
-                strip = now[planes + q]
-                mixed = strip
-                for g in range(nz):
-                    slot = q * nz + g
-                    j = slot if q == 0 else 3 * nz - 1 - slot
-                    if j <= last:
-                        mixed = jnp.where(
-                            group_of == g, lane_roll(now[slot], GROUP * g + 8), mixed
-                        )
-                after = lane_roll(jnp.where(inner_held == 8, mixed, strip), -1)
-                before = lane_roll(jnp.where(inner_held == 7, mixed, strip), 1)
-                moved[0, planes + q], moved[1, planes + q] = after, before
-                triples.append((strip, after, before))
-            for number in range(3):
-                found = across(triples[0][number], triples[1][number])
-                for which, value in enumerate(found):
-                    beside[which, number] = value
-            for q in range(2):
-                slot = planes + q
-
-                def near(dz, dy):
-                    number = {0: 0, 1: 1, -1: 2}[dy]
-                    if dz:
-                        return beside.at[q if dz == 1 else 2 + q, number]
-                    return now.at[slot] if dy == 0 else moved.at[number - 1, slot]
-
-                advance(step, slot, near, slice(0, held), first)
+        entering = min(last + 1, planes)
+        rings = {}
+
+        def turn(j):
+            if LEAD <= j < entering:
+                rings[j] = ring_plane(now, j)
+
+        def roll(j):
+            if LEAD <= j < entering:
+                roll_plane(now, j, rings.pop(j))
+
+        mixed, triples = {}, {}
+
+        def insert(q):
+            total = now[planes + q]
+            for g in range(nz):
+                slot = q * nz + g
+                j = slot if q == 0 else 3 * nz - 1 - slot
+                if j <= last:
+                    total = jnp.where(group_of == g, lane_roll(now[slot], GROUP * g + 8), total)
+            mixed[q] = total
+
+        def shift_strip(q):
+            strip = now[planes + q]
+            after = lane_roll(jnp.where(inner_held == 8, mixed[q], strip), -1)
+            before = lane_roll(jnp.where(inner_held == 7, mixed[q], strip), 1)
+            moved[0, planes + q], moved[1, planes + q] = after, before
+
+        def cross(number):
+            if number:
+                found = across(moved[number - 1, planes], moved[number - 1, planes + 1])
+            else:
+                found = across(now[planes], now[planes + 1])
+            for which, value in enumerate(found):
+                beside[which, number] = value
+
+        def advance_strip(q):
+            slot = planes + q
+
+            def near(dz, dy):
+                number = {0: 0, 1: 1, -1: 2}[dy]
+                if dz:
+                    return beside.at[q if dz == 1 else 2 + q, number]
+                return now.at[slot] if dy == 0 else moved.at[number - 1, slot]
+
+            advance(step, slot, near, slice(0, held), first)
+
+        coming = basis.at[step]
+        plan = {
+            0: [lambda: insert(0)],
+            1: [lambda: insert(1)],
+            2: [lambda: shift_strip(0), lambda: shift_strip(1)],
+            3: [lambda: cross(0)],
+            4: [lambda: cross(1)],
+            5: [lambda: cross(2)],
+            7: [lambda: advance_strip(0), lambda: advance_strip(1)],
+            9: [lambda: rings.update({-1 - j: ring_plane(coming, j) for j in range(LEAD)})],
+            10: [lambda: roll_plane(coming, 0, rings[-1]), lambda: roll_plane(coming, 1, rings[-2])],
+            11: [lambda: roll_plane(coming, 2, rings[-3]), lambda: roll_plane(coming, 3, rings[-4])],
+        }
         sums = [zero8, zero8, zero8]
+        turn(LEAD)
         for j in range(last):
+            turn(j + LEAD + 1)
+            roll(j + LEAD)
+            if not final:
+                for work in plan.get(j, []):
+                    work()
             slot = at(j)
 
             def near(dz, dy):
@@ -1081,6 +1133,8 @@
         one_step(step, planes - 4)
         return carry
 
+    for j in range(LEAD):
+        roll_plane(basis.at[0], j, ring_plane(basis.at[0], j))
     lax.fori_loop(1, 4, early_steps, 0)
     lax.fori_loop(4, ITERS, later_steps, 0)
     one_step(ITERS, nz, final=True)
@@ -1203,7 +1257,7 @@
         pltpu.SMEM((nz,), jnp.int32), pltpu.SMEM((nz,), jnp.int32), pltpu.SMEM((planes,), jnp.int32),
         pltpu.SemaphoreType.DMA((4,)), pltpu.SemaphoreType.DMA((moves,)),
         pltpu.SemaphoreType.DMA((moves,)), pltpu.SemaphoreType.DMA((3,)),
-        pltpu.SemaphoreType.DMA((3,)),
+        pltpu.SemaphoreType.DMA((3,)), pltpu.SemaphoreType.REGULAR,
     ]
     shapes = (jax.ShapeDtypeStruct(extent, jnp.float32),) * 2
     found = pl.pallas_call(
@@ -1232,7 +1286,7 @@
     nz, nx, ny = tissue_mask.shape
     fits = (
         lax.axis_size("gz") == 2 and nz == 8 and ITERS == 8 and nx % 8 == 0 and nx >= 16
-        and ny == nz * GROUP and lax.axis_size("gx") > 1 and lax.axis_size("gy") > 1
+        and ny == nz * GROUP and 1 < lax.axis_size("gx") <= 4 and lax.axis_size("gy") > 1
     )
     return (fast_body if fits else general_body)(potential, tissue_mask, layer_index, source)
 

time: 29.6 us -> 28.8 us (0.973)
  Pallas kernels: 28.8 us -> 28 us
    pallas_call x1, Pallas kernels: 28.1 us -> 27.3 us  [fast_body(): pl.pallas_call(functools.partial(fast_kernel, extent, sizes), out_shape=s...]
where the time goes in v5:
time: 28.8 us; the launch traced here: 28.6 us
  Pallas kernels  28 us (97%)
  between operations  0.64 us (2%)
    pallas_call x1, Pallas kernels, fast_body(): pl.pallas_call(functools.partial(fast_kernel, extent, sizes), out_shape=s...  27.3 us
    pallas_call x1, Pallas kernels, fast_body(): pl.pallas_call(hand_out, out_shape=shapes, in_specs=[vmem] * 2, out_specs...  0.69 us

profile of v5, /device:TPU:0, one launch (start us, length us, event | category | flops | bytes accessed | tf_op | source)
XLA Modules:
  0.0 28.6 jit_solution(17490200827254223675)
XLA Ops:
  0.6 27.3 %shard_map.59 = (f32[8,24,128]{2,1,0:T(8,128)S(1)}, f32[8,24,128]{2,1,0:T(8,128)S(1)}) custom-call(f32[8,24,128]{2,1,0:T(8,128)} %potential_in.1, s32[8,24,128]{2,1,0:T(8,128)} %mask_in.1, s32[8]{0:T(128)} %layers_in.1, f32[8,24,128]{2,1,0:T(8,128)} %source_in.1), custom_call_target="tpu_custom_call" | custom-call | tf_op jit(solution)/shard_map/pallas_call | solution.py:1263
  27.9 0.7 %shard_map.60 = (f32[8,24,128]{2,1,0:T(8,128)}, f32[8,24,128]{2,1,0:T(8,128)}) custom-call(f32[8,24,128]{2,1,0:T(8,128)S(1)} %get-tuple-element.4.phi, f32[8,24,128]{2,1,0:T(8,128)S(1)} %get-tuple-element.5.residual), custom_call_target="tpu_custom_call" | custom-call | tf_op jit(solution)/shard_map/pallas_call | solution.py:1274

commit v6 on v5

--- a/solution.py
+++ b/solution.py
@@ -522,8 +522,22 @@
 
     get_layers = pltpu.make_async_copy(layers_in, layers_own, loads.at[0])
     get_mask = pltpu.make_async_copy(mask_in, labels, loads.at[1])
+    get_mask.start()
     get_layers.start()
-    get_mask.start()
+    barrier = pltpu.get_barrier_semaphore()
+
+    def greet(target):
+        pl.semaphore_signal(
+            barrier, inc=1, device_id=target, device_id_type=pl.DeviceIdType.MESH
+        )
+
+    expected = len(slab) - 1
+    for dx, dy in corners + [(1, 0), (-1, 0)]:
+        pl.when(exists(dx, dy))(lambda: greet((gx + dx, gy + dy, side)))
+        expected = expected + jnp.where(exists(dx, dy), 1, 0)
+    for step in slab[1:]:
+        greet(around(*step))
+
     whole = []
     for index, ref in ((1, potential_in), (2, source_in)):
         for plane in range(nz):
@@ -531,20 +545,6 @@
                 ref.at[plane], fields.at[index, flip(plane, side), own], loads.at[1 + index]
             ).start()
         whole.append(pltpu.make_async_copy(ref, fields.at[index, 0:nz, own], loads.at[1 + index]))
-
-    barrier = pltpu.get_barrier_semaphore()
-
-    def greet(target):
-        pl.semaphore_signal(
-            barrier, inc=1, device_id=target, device_id_type=pl.DeviceIdType.MESH
-        )
-
-    expected = len(slab) - 1
-    for dx, dy in corners + [(1, 0), (-1, 0)]:
-        pl.when(exists(dx, dy))(lambda: greet((gx + dx, gy + dy, side)))
-        expected = expected + jnp.where(exists(dx, dy), 1, 0)
-    for step in slab[1:]:
-        greet(around(*step))
 
     def clear(when, ref, index):
         @pl.when(when)
@@ -998,25 +998,37 @@
 
     lane_of, group_of, inner_held = lanes_of(held)
 
+    tiles = held // 8
+
     def advance(step, slot, near, rows, first):
-        same = None
-        for number, (dz, dy) in enumerate(TERMS_SAME):
-            value = near(dz, dy)
-            if value is None:
-                continue
-            term = weights[number, slot, rows] * value[rows]
-            same = term if same is None else same + term
-        for dx, begin in ((1, 8), (-1, 13)):
-            part = None
-            for number, (dz, dy) in enumerate(TERMS_SIDE):
-                value = near(dz, dy)
-                if value is None:
-                    continue
-                term = weights[begin + number, slot] * value[...]
-                part = term if part is None else part + term
-            same = same + row_roll(part, -dx)[rows]
+        kept = range(rows.start // 8, rows.stop // 8)
+        same, plus, minus = [None] * tiles, [None] * tiles, [None] * tiles
+        for t in range(max(kept.start - 1, 0), min(kept.stop + 1, tiles)):
+            spot = slice(8 * t, 8 * t + 8)
+            values = {}
+            for key in TERMS_SIDE + TERMS_SAME:
+                ref = near(*key)
+                if ref is not None:
+                    values[key] = ref[spot]
+            for found, terms, begin_at, wanted in (
+                (same, TERMS_SAME, 0, t in kept),
+                (plus, TERMS_SIDE, 8, t >= kept.start),
+                (minus, TERMS_SIDE, 13, t < kept.stop),
+            ):
+                for number, key in enumerate(terms):
+                    if wanted and key in values:
+                        term = weights[begin_at + number, slot, spot] * values[key]
+                        found[t] = term if found[t] is None else found[t] + term
+
+        def shifted_rows(found, step_by):
+            filler = next(value for value in found if value is not None)
+            whole = jnp.concatenate([filler if value is None else value for value in found], axis=0)
+            return row_roll(whole, step_by)[rows]
+
+        total = jnp.concatenate([same[t] for t in kept], axis=0)
+        total = total + shifted_rows(plus, -1) + shifted_rows(minus, 1)
         value = basis[step - 1, slot, rows]
-        fresh = jac[slot, rows] * same + spare[slot, rows] * value
+        fresh = jac[slot, rows] * total + spare[slot, rows] * value
         if first:
             factor = jnp.where(step == 1, 0.5, 1.0).astype(jnp.float32)
             back = jnp.where(step == 1, 0.0, 1.0).astype(jnp.float32)
@@ -1026,7 +1038,7 @@
         basis[step, slot, rows] = fresh
         return fresh, value
 
-    LEAD = 4
+    LEAD = 3
 
     def roll_plane(field, j, ring):
         slot = at(j)
@@ -1088,15 +1100,18 @@
         coming = basis.at[step]
         plan = {
             0: [lambda: insert(0)],
-            1: [lambda: insert(1)],
-            2: [lambda: shift_strip(0), lambda: shift_strip(1)],
-            3: [lambda: cross(0)],
-            4: [lambda: cross(1)],
-            5: [lambda: cross(2)],
-            7: [lambda: advance_strip(0), lambda: advance_strip(1)],
-            9: [lambda: rings.update({-1 - j: ring_plane(coming, j) for j in range(LEAD)})],
-            10: [lambda: roll_plane(coming, 0, rings[-1]), lambda: roll_plane(coming, 1, rings[-2])],
-            11: [lambda: roll_plane(coming, 2, rings[-3]), lambda: roll_plane(coming, 3, rings[-4])],
+            1: [lambda: shift_strip(0), lambda: insert(1)],
+            2: [lambda: shift_strip(1), lambda: cross(0)],
+            3: [lambda: cross(1)],
+            4: [lambda: cross(2)],
+            6: [lambda: advance_strip(0), lambda: advance_strip(1)],
+            8: [lambda: rings.update({-1 - j: ring_plane(coming, j) for j in (0, 1)})],
+            9: [
+                lambda: roll_plane(coming, 0, rings[-1]),
+                lambda: roll_plane(coming, 1, rings[-2]),
+                lambda: rings.update({-3: ring_plane(coming, 2)}),
+            ],
+            10: [lambda: roll_plane(coming, 2, rings[-3])],
         }
         sums = [zero8, zero8, zero8]
         turn(LEAD)

time: 28.8 us -> 28.3 us (0.983)
  Pallas kernels: 28 us -> 27.5 us
    pallas_call x1, Pallas kernels: 27.3 us -> 26.9 us  [fast_body(): pl.pallas_call(functools.partial(fast_kernel, extent, sizes), out_shape=s...]
where the time goes in v6:
time: 28.3 us; the launch traced here: 28.2 us
  Pallas kernels  27.5 us (97%)
  between operations  0.64 us (2%)
    pallas_call x1, Pallas kernels, fast_body(): pl.pallas_call(functools.partial(fast_kernel, extent, sizes), out_shape=s...  26.9 us
    pallas_call x1, Pallas kernels, fast_body(): pl.pallas_call(hand_out, out_shape=shapes, in_specs=[vmem] * 2, out_specs...  0.69 us

profile of v6, /device:TPU:0, one launch (start us, length us, event | category | flops | bytes accessed | tf_op | source)
XLA Modules:
  0.0 28.2 jit_solution(8802234905180389799)
XLA Ops:
  0.6 26.9 %shard_map.59 = (f32[8,24,128]{2,1,0:T(8,128)S(1)}, f32[8,24,128]{2,1,0:T(8,128)S(1)}) custom-call(f32[8,24,128]{2,1,0:T(8,128)} %potential_in.1, s32[8,24,128]{2,1,0:T(8,128)} %mask_in.1, s32[8]{0:T(128)} %layers_in.1, f32[8,24,128]{2,1,0:T(8,128)} %source_in.1), custom_call_target="tpu_custom_call" | custom-call | tf_op jit(solution)/shard_map/pallas_call | solution.py:1278
  27.5 0.7 %shard_map.60 = (f32[8,24,128]{2,1,0:T(8,128)}, f32[8,24,128]{2,1,0:T(8,128)}) custom-call(f32[8,24,128]{2,1,0:T(8,128)S(1)} %get-tuple-element.4.phi, f32[8,24,128]{2,1,0:T(8,128)S(1)} %get-tuple-element.5.residual), custom_call_target="tpu_custom_call" | custom-call | tf_op jit(solution)/shard_map/pallas_call | solution.py:1289

commit v7 on v6

--- a/solution.py
+++ b/solution.py
@@ -966,7 +966,12 @@
     mixed = lax.fori_loop(0, nz // 2, own_begin, strips[2, 1])
     derive_strip(1, 1, mixed)
     derive_beside(1)
-    lax.fori_loop(nz - 1, planes, plane_begin, 0)
+    def three_begin(block, carry):
+        for m in range(3):
+            plane_begin(nz - 1 + 3 * block + m, 0)
+        return carry
+
+    lax.fori_loop(0, (nz + 1) // 3, three_begin, 0)
     lax.fori_loop(0, 2, strip_begin, 0)
 
     def folded(value):
@@ -1118,9 +1123,6 @@
         for j in range(last):
             turn(j + LEAD + 1)
             roll(j + LEAD)
-            if not final:
-                for work in plan.get(j, []):
-                    work()
             slot = at(j)
 
             def near(dz, dy):
@@ -1138,6 +1140,9 @@
                 sums[0] = sums[0] + folded(weighted * fresh)
                 sums[1] = sums[1] + folded(weighted * value)
                 sums[2] = sums[2] + folded(fresh)
+            if not final:
+                for work in plan.get(j, []):
+                    work()
         record(step, sums)
 
     def early_steps(step, carry):

time: 28.3 us -> 28.3 us (level)
  no operation moved by 1% of the time
where the time goes in v7:
time: 28.3 us; the launch traced here: 28.1 us
  Pallas kernels  27.5 us (97%)
  between operations  0.64 us (2%)
    pallas_call x1, Pallas kernels, fast_body(): pl.pallas_call(functools.partial(fast_kernel, extent, sizes), out_shape=s...  26.8 us
    pallas_call x1, Pallas kernels, fast_body(): pl.pallas_call(hand_out, out_shape=shapes, in_specs=[vmem] * 2, out_specs...  0.69 us

profile of v7, /device:TPU:0, one launch (start us, length us, event | category | flops | bytes accessed | tf_op | source)
XLA Modules:
  0.0 28.1 jit_solution(4609274746532582309)
XLA Ops:
  0.6 26.8 %shard_map.59 = (f32[8,24,128]{2,1,0:T(8,128)S(1)}, f32[8,24,128]{2,1,0:T(8,128)S(1)}) custom-call(f32[8,24,128]{2,1,0:T(8,128)} %potential_in.1, s32[8,24,128]{2,1,0:T(8,128)} %mask_in.1, s32[8]{0:T(128)} %layers_in.1, f32[8,24,128]{2,1,0:T(8,128)} %source_in.1), custom_call_target="tpu_custom_call" | custom-call | tf_op jit(solution)/shard_map/pallas_call | solution.py:1283
  27.5 0.7 %shard_map.60 = (f32[8,24,128]{2,1,0:T(8,128)}, f32[8,24,128]{2,1,0:T(8,128)}) custom-call(f32[8,24,128]{2,1,0:T(8,128)S(1)} %get-tuple-element.4.phi, f32[8,24,128]{2,1,0:T(8,128)S(1)} %get-tuple-element.5.residual), custom_call_target="tpu_custom_call" | custom-call | tf_op jit(solution)/shard_map/pallas_call | solution.py:1294
